TPU v7x, 32 devices: a whole 2x2x4 slice. The times are simulated.
32 devices in a mesh: batch: 4 (over y, x), proto: 8 (over z, core).
Axes of the slice: x: 2, y: 2, z: 4, core: 2. Of those that a mesh axis runs over, the one named last changes fastest.
Arguments:
- view_codes: bfloat16 [4096, 1024], P('batch', 'proto'), may hold values from -80 to 80
- predictor_view_embeddings: bfloat16 [4096, 1024], P('batch', 'proto'), may hold values from -80 to 80
- prototypes: bfloat16 [65536, 1024], P('proto'), may hold values from -64 to 64
Outputs:
- assignments: bfloat16 [4096, 65536], P('batch', 'proto')
- loss_rows: float32 [4096], P('batch')
All inputs are finite; a program needn't handle non-finite values.
Results may differ from a plain program's by a relative error of at most 0.0034.
Values may be sent and summed in bfloat16 or wider, within the bound.
No kernel may reach another device: no remote copies, remote signals or barrier semaphores. Data moves between devices by JAX's collectives and lax.ppermute only.
A program may use at most 128 MiB of HBM per device.

v0:
```python
import jax
import jax.numpy as jnp
from jax import lax
from jax.sharding import PartitionSpec as P

SINK_ITERS = 3


EPSILON = 0.05
SOFTMAX_TEMP_VALUE = 0.1


def normalized(prototypes):
    weights = prototypes.astype(jnp.float32)
    return (weights * lax.rsqrt(jnp.sum(weights * weights, axis=1, keepdims=True) + 1e-06)).astype(
        jnp.bfloat16
    )


def view_scores(embedded, unit_prototype_rows):
    products = jnp.dot(embedded, unit_prototype_rows.T, preferred_element_type=jnp.float32)
    values = embedded.astype(jnp.float32)
    inverse_factor = lax.rsqrt(jnp.sum(values * values, axis=1) + 1e-06)
    return products * inverse_factor[:, None]


def local(view_codes, predictor_view_embeddings, prototypes):
    unit_prototype_rows = normalized(prototypes)
    first_view_local, local_second = (
        lax.all_to_all(view_codes, "proto", split_axis=0, concat_axis=1, tiled=True),
        lax.all_to_all(predictor_view_embeddings, "proto", split_axis=0, concat_axis=1, tiled=True),
    )
    stacked = jnp.stack([first_view_local, local_second])
    piece = lax.all_gather(stacked, "proto", axis=1, tiled=True)
    scored = jnp.stack(
        [view_scores(piece[0], unit_prototype_rows), view_scores(piece[1], unit_prototype_rows)]
    )
    scores_codes = scored[0]
    predictor_scores = scored[1]
    kernel = jnp.exp(scores_codes / EPSILON)
    rows_total = kernel.shape[0] * lax.axis_size("batch")
    protos_total = kernel.shape[1] * lax.axis_size("proto")
    logit_scores = predictor_scores / SOFTMAX_TEMP_VALUE
    totals = lax.psum(jnp.sum(jnp.exp(logit_scores), axis=1), "proto")
    scale_rows = jnp.ones((kernel.shape[0],), jnp.float32)
    for iteration in range(SINK_ITERS):
        col_part = jnp.dot(scale_rows, kernel, precision=lax.Precision.HIGHEST)
        col_sums = lax.psum(col_part, "batch")
        scale_cols = 1.0 / (protos_total * col_sums)
        row_part = jnp.dot(kernel, scale_cols, precision=lax.Precision.HIGHEST)
        row_sums = lax.psum(row_part, "proto")
        scale_rows = 1.0 / (rows_total * row_sums)
    assign = kernel * scale_cols[None, :] * (rows_total * scale_rows)[:, None]
    assignments = (protos_total * assign).astype(jnp.bfloat16)
    cross_part = jnp.sum(assign * logit_scores, axis=1)
    cross_term = lax.psum(cross_part, "proto")
    loss_rows = jnp.log(totals) - cross_term
    return (assignments, loss_rows)


def solution(mesh):
    placed = (P("batch", "proto"), P("batch", "proto"), P("proto", None))
    return jax.shard_map(
        local,
        mesh=mesh,
        in_specs=placed,
        out_specs=(P("batch", "proto"), P("batch")),
        check_vma=False,
    )
```

profile of v0, /device:TPU:0, one launch (start us, length us, event | category | flops | bytes accessed | tf_op | source)
XLA Modules:
  0.0 412.2 jit_solution(1845674202562037767)
XLA Ops:
  7.2 16.1 %all_to_all.32 = bf16[8,128,128]{2,1,0:T(8,128)(2,1)S(1)} all-to-all(bf16[8,128,128]{2,1,0:T(8,128)(2,1)} %bitcast.44), channel_id=1, replica_groups=mesh['batch'=4,'proto'=8] {'proto'}, dimensions={0} | all-to-all | bytes 524288 | tf_op jit(solution)/shard_map/all_to_all | solution.py:30
  23.2 3.4 all-to-all-start.1
  26.7 0.0 all-gather.2.cloned.1.call-start
  26.7 0.2 copy.5
  26.9 9.4 %all-to-all-done.1 = bf16[8,128,128]{2,1,0:T(8,128)(2,1)S(1)} async-done(((bf16[8,128,128]{2,1,0:T(8,128)(2,1)}), bf16[8,128,128]{2,1,0:T(8,128)(2,1)S(1)}, u32[]{:S(2)}, u32[]{:S(2)}) %all-to-all-start.1) | async-done | bytes 262176 | tf_op jit(solution)/shard_map/all_to_all | solution.py:31
  36.3 0.2 copy.6
  36.5 0.8 pad_maximum_fusion
  37.3 0.0 all-gather.2.cloned.1.call-update
  37.3 7.4 %fusion = f32[8192]{0:T(1024)S(1)} fusion(bf16[8192,1024]{1,0:T(8,128)(2,1)} %param.5), kind=kLoop, calls=%fused_computation.2 | loop fusion | flops 25157632 | bytes 16809984 | tf_op jit(solution)/shard_map/reduce_sum | solution.py:15
  44.7 39.5 %all-gather.2.cloned.1.call-done = bf16[2,1024,1024]{1,2,0:T(8,128)(2,1)} async-done(((bf16[2,128,1024]{1,2,0:T(8,128)(2,1)}), bf16[2,1024,1024]{1,2,0:T(8,128)(2,1)}) %all-gather.2.cloned.1.call-update) | async-done | bytes 4194320 | tf_op jit(solution)/shard_map/all_gather | solution.py:34
  84.2 3.3 multiply_reduce_fusion.1
  87.6 28.6 %multiply_exponential_fusion = f32[1024,8192]{1,0:T(8,128)} fusion(f32[1024]{0:T(1024)S(1)} %add_rsqrt_fusion.2, bf16[8192,1024]{1,0:T(8,128)(2,1)} %param.5, f32[8192]{0:T(1024)S(1)} %add_rsqrt_fusion, bf16[2,1024,1024]{1,2,0:T(8,128)(2,1)} %all-gather.2.cloned.1.call-done), kind=kOutput, calls=%fused_computation.9 | convolution fusion | flops 17221812224 | bytes 52465664 | tf_op jit(solution)/shard_map/dot_general | solution.py:21
  116.2 19.9 %fusion.5 = f32[1,8192]{1,0:T(1,128)S(1)} fusion(f32[1024,8192]{1,0:T(8,128)} %multiply_exponential_fusion), kind=kOutput, calls=%fused_computation.26 | convolution fusion | flops 100663296 | bytes 33587200 | tf_op jit(solution)/shard_map/dot_general | solution.py:47
  136.1 16.2 %psum.56 = f32[8192]{0:T(1024)S(1)} all-reduce(f32[8192]{0:T(1024)S(1)} %bitcast.51), channel_id=1, replica_groups=mesh['batch'=4,'proto'=8] {'batch'}, use_global_device_ids=true, to_apply=%region_2.0 | all-reduce | flops 8192 | bytes 65536 | tf_op jit(solution)/shard_map/psum | solution.py:48
  152.4 31.7 %fusion.8 = f32[1,1024]{1,0:T(1,128)S(1)} fusion(f32[1024,8192]{1,0:T(8,128)} %multiply_exponential_fusion, f32[8192,1]{0,1:T(1,128)S(1)} %bitcast.49), kind=kOutput, calls=%fused_computation.29 | convolution fusion | flops 100663296 | bytes 33591296 | tf_op jit(solution)/shard_map/dot_general | solution.py:50
  184.1 13.6 %psum.57 = f32[1024]{0:T(1024)S(1)} all-reduce(f32[1024]{0:T(1024)S(1)} %bitcast.52), channel_id=1, replica_groups=mesh['batch'=4,'proto'=8] {'proto'}, use_global_device_ids=true, to_apply=%region_3.0 | all-reduce | flops 1024 | bytes 8192 | tf_op jit(solution)/shard_map/psum | solution.py:51
  197.7 19.7 %fusion.9 = f32[1,8192]{1,0:T(1,128)S(1)} fusion(f32[1024,1]{0,1:T(1,128)S(1)} %bitcast.55, f32[1024,8192]{1,0:T(8,128)} %multiply_exponential_fusion), kind=kOutput, calls=%fused_computation.30 | convolution fusion | flops 100663296 | bytes 33591296 | tf_op jit(solution)/shard_map/dot_general | solution.py:47
  217.4 14.3 %psum.58 = f32[8192]{0:T(1024)S(1)} all-reduce(f32[8192]{0:T(1024)S(1)} %bitcast.46), channel_id=1, replica_groups=mesh['batch'=4,'proto'=8] {'batch'}, use_global_device_ids=true, to_apply=%region_4.0 | all-reduce | flops 8192 | bytes 65536 | tf_op jit(solution)/shard_map/psum | solution.py:48
  231.7 31.7 %fusion.10 = f32[1,1024]{1,0:T(1,128)S(1)} fusion(f32[1024,8192]{1,0:T(8,128)} %multiply_exponential_fusion, f32[8192,1]{0,1:T(1,128)S(1)} %bitcast.50), kind=kOutput, calls=%fused_computation.31 | convolution fusion | flops 100663296 | bytes 33591296 | tf_op jit(solution)/shard_map/dot_general | solution.py:50
  263.4 13.6 %psum.59 = f32[1024]{0:T(1024)S(1)} all-reduce(f32[1024]{0:T(1024)S(1)} %bitcast.53), channel_id=1, replica_groups=mesh['batch'=4,'proto'=8] {'proto'}, use_global_device_ids=true, to_apply=%region_5.0 | all-reduce | flops 1024 | bytes 8192 | tf_op jit(solution)/shard_map/psum | solution.py:51
  277.0 19.7 %fusion.11 = f32[1,8192]{1,0:T(1,128)S(1)} fusion(f32[1024,1]{0,1:T(1,128)S(1)} %bitcast.56, f32[1024,8192]{1,0:T(8,128)} %multiply_exponential_fusion), kind=kOutput, calls=%fused_computation.32 | convolution fusion | flops 100663296 | bytes 33591296 | tf_op jit(solution)/shard_map/dot_general | solution.py:47
  296.7 15.4 %psum.60 = f32[8192]{0:T(1024)S(1)} all-reduce(f32[8192]{0:T(1024)S(1)} %bitcast.47), channel_id=1, replica_groups=mesh['batch'=4,'proto'=8] {'batch'}, use_global_device_ids=true, to_apply=%region_6.0 | all-reduce | flops 8192 | bytes 65536 | tf_op jit(solution)/shard_map/psum | solution.py:48
  312.2 31.7 %fusion.12 = f32[1,1024]{1,0:T(1,128)S(1)} fusion(f32[1024,8192]{1,0:T(8,128)} %multiply_exponential_fusion, f32[8192,1]{0,1:T(1,128)S(1)} %bitcast.48), kind=kOutput, calls=%fused_computation.33 | convolution fusion | flops 100663296 | bytes 33591296 | tf_op jit(solution)/shard_map/dot_general | solution.py:50
  343.9 13.6 %psum.61 = f32[1024]{0:T(1024)S(1)} all-reduce(f32[1024]{0:T(1024)S(1)} %bitcast.54), channel_id=1, replica_groups=mesh['batch'=4,'proto'=8] {'proto'}, use_global_device_ids=true, to_apply=%region_7.0 | all-reduce | flops 1024 | bytes 8192 | tf_op jit(solution)/shard_map/psum | solution.py:51
  357.5 32.9 %exponential_reduce_fusion = (f32[1024]{0:T(1024)S(1)}, f32[1024]{0:T(1024)S(1)}, bf16[1024,8192]{1,0:T(8,128)(2,1)}) fusion(f32[1024]{0:T(1024)S(1)} %add_rsqrt_fusion.1, f32[1024]{0:T(1024)S(1)} %divide_multiply_fusion, f32[1024,8192]{1,0:T(8,128)} %multiply_exponential_fusion, f32[8192]{0:T(1024)S(1)} %multiply_divide_fusion, ...), kind=kOutput, calls=%fused_computation.5 | convolution fusion | flops 17280532480 | bytes 69287936 | tf_op jit(solution)/shard_map/dot_general | solution.py:21
  390.4 13.9 %all-reduce = (f32[1024]{0:T(1024)S(1)}, f32[1024]{0:T(1024)S(1)}) all-reduce(f32[1024]{0:T(1024)S(1)} %get-tuple-element.3, f32[1024]{0:T(1024)S(1)} %get-tuple-element.2), channel_id=1, replica_groups=mesh['batch'=4,'proto'=8] {'proto'}, use_global_device_ids=true, to_apply=%region_12.0 | all-reduce | flops 2048 | bytes 16384 | tf_op jit(solution)/shard_map/psum | solution.py:56
  404.3 0.6 log_subtract_fusion
  (9 shorter events, 0.1 us)
Async XLA Ops:
  23.2 13.1 %all-to-all-start.1 = ((bf16[8,128,128]{2,1,0:T(8,128)(2,1)}), bf16[8,128,128]{2,1,0:T(8,128)(2,1)S(1)}, u32[]{:S(2)}, u32[]{:S(2)}) async-start(bf16[8,128,128]{2,1,0:T(8,128)(2,1)} %bitcast.45), calls=%async_computation.1 | async-start | bytes 524288 | tf_op jit(solution)/shard_map/all_to_all | solution.py:31
  26.7 57.6 %all-gather.2.cloned.1.call-start = ((), (), s32[]{:S(2)}) async-start(), calls=%async_computation.2 | async-start | bytes 4718592 | tf_op jit(solution)/shard_map/all_gather | solution.py:34
Sparse Core Ops, SparseCore 0:
  37.5 46.7 all-gather.1
where the time goes:
time: 419 us; the launch traced here: 412 us
  matrix products  216 us (52%)
  blocking collectives  117 us (28%)
  waiting for transfers between devices  48.9 us (12%)
  between operations  14.6 us (3%)
  other arithmetic  12.2 us (3%)
    dot_general x3, matrix products, local(): row_part = jnp.dot(kernel, scale_cols, precision=lax.Precision.HIGHEST)  95.2 us
    dot_general x2, matrix products, view_scores(): jnp.dot(embedded, unit_prototype_rows.T, preferred_element_type=jnp.float32)  61.5 us
    dot_general x3, matrix products, local(): col_part = jnp.dot(scale_rows, kernel, precision=lax.Precision.HIGHEST)  59.3 us
    psum x3, blocking collectives, local(): col_sums = lax.psum(col_part, 'batch')  45.9 us
    psum x3, blocking collectives, local(): row_sums = lax.psum(row_part, 'proto')  40.8 us
    all_gather x1, waiting for transfers between devices, local(): piece = lax.all_gather(stacked, 'proto', axis=1, tiled=True)  39.5 us
    all_to_all x1, blocking collectives, local(): lax.all_to_all(view_codes, 'proto', split_axis=0, concat_axis=1, tiled=True)  16.1 us
    psum x1, blocking collectives, local(): cross_term = lax.psum(cross_part, 'proto')  13.9 us
  transfers between devices with their start and end apart: 2, of which 2 were waited for; matrix products, arithmetic and copies ran while one was open for 2% of the time, Pallas kernels for 0%

commit v1 on v0

v1 whole, which is shorter than its diff:
```python
import functools

import jax
import jax.numpy as jnp
from jax import lax
from jax.experimental import pallas as pl
from jax.experimental.pallas import tpu as pltpu
from jax.sharding import PartitionSpec as P

SINK_ITERS = 3
EPSILON = 0.05
SOFTMAX_TEMP_VALUE = 0.1
NORM_EPS = 1e-06
CHUNKS = 4
HALVES = 4
PIECES = 8
NEAR = 2 * CHUNKS
COVER = (2, 2, 2, 1, 1)
LANES = 128
LOG2E = 1.4426950408889634
LOGIT_STEPS = 2200.0


F32 = jnp.float32
BF16 = jnp.bfloat16
VM = pl.BlockSpec(memory_space=pltpu.VMEM)
HB = pl.BlockSpec(memory_space=pltpu.HBM)


def call(kernel, outs, ins, args, scratch=(), limit=6, flops=0, alias=None):
    big = lambda a: a.size * a.dtype.itemsize > (4 << 20)
    args = [
        pltpu.with_memory_space_constraint(a, pltpu.HBM if spec is HB else pltpu.VMEM) if spec is HB or big(a) else a
        for a, spec in zip(args, ins)
    ]
    return pl.pallas_call(
        kernel,
        out_shape=outs,
        in_specs=ins,
        out_specs=jax.tree.map(
            lambda o: HB if getattr(o, "memory_space", None) == pltpu.HBM else VM, outs
        ),
        scratch_shapes=list(scratch),
        input_output_aliases=alias or {},
        compiler_params=pltpu.CompilerParams(vmem_limit_bytes=limit << 20),
        cost_estimate=pl.CostEstimate(flops=int(flops), bytes_accessed=0, transcendentals=0),
    )(*args)


def rows_to_lanes(block):
    out = []
    for i in range(block.shape[0] // LANES):
        part = block[i * LANES : (i + 1) * LANES, :]
        out.append(jnp.sum(part.T, axis=0, keepdims=True))
    return jnp.concatenate(out, axis=0)


def lanes_to_rows(packed, out_ref):
    for i in range(packed.shape[0]):
        row = jnp.broadcast_to(packed[i : i + 1, :], (LANES, LANES))
        out_ref[i * LANES : (i + 1) * LANES, :] = row.T


def fetch(src, buf, sems, tile, i, slot):
    rows = pl.ds(pl.multiple_of(i * tile, tile), tile)
    return pltpu.make_async_copy(src.at[rows, :], buf.at[slot], sems.at[slot])


def norm_kernel(tile, depth, p_ref, u_ref, buf, obuf, inv, sems, osems):
    total = p_ref.shape[0]
    steps = total // tile
    width = p_ref.shape[1] // CHUNKS
    load = lambda i, slot: fetch(p_ref, buf, sems, tile, i, slot)

    def store(i, slot):
        rows = pl.ds(pl.multiple_of(i * tile, tile), tile)
        return pltpu.make_async_copy(obuf.at[slot], u_ref.at[:, rows, :], osems.at[slot])

    for i in range(min(depth, steps)):
        load(i, i).start()
    sub = min(32, tile)

    def step(i, carry):
        slot = lax.rem(i, depth)
        load(i, slot).wait()

        @pl.when(i >= depth)
        def _():
            store(i - depth, slot).wait()

        def sums(t, c):
            rows = pl.ds(pl.multiple_of(t * sub, sub), sub)
            x = buf[slot, rows, :].astype(F32)
            total = jnp.sum(x * x, axis=1, keepdims=True)
            inv[rows, :] = jnp.broadcast_to(lax.rsqrt(total + NORM_EPS), (sub, LANES))
            return c

        def scale(t, c):
            rows = pl.ds(pl.multiple_of(t * sub, sub), sub)
            r = inv[rows, :]
            for l in range(CHUNKS * width // LANES):
                x = buf[slot, rows, l * LANES : (l + 1) * LANES].astype(F32)
                at = l * LANES % width
                obuf[slot, l * LANES // width, rows, at : at + LANES] = (x * r).astype(BF16)
            return c

        lax.fori_loop(0, tile // sub, sums, 0, unroll=8)
        lax.fori_loop(0, tile // sub, scale, 0, unroll=2)
        store(i, slot).start()

        @pl.when(i + depth < steps)
        def _():
            load(i + depth, slot).start()

        return carry

    lax.fori_loop(0, steps, step, 0)
    for i in range(max(steps - depth, 0), steps):
        store(i, i % depth).wait()


def order(fast, core, own, sib):
    if not fast:
        return own, sib
    return jnp.where(core == 0, own, sib), jnp.where(core == 0, sib, own)


def position(fast):
    if not fast:
        return 0, 0
    me = lax.axis_index("proto")
    return lax.div(me, 2), lax.rem(me, 2)


def square(x):
    y = x.astype(F32)
    return y * y


def stage_kernel(fast, slots, last, scale, tile, block, *refs):
    count = len(slots)
    own = refs[:count]
    sib = refs[count : 2 * count]
    unit = refs[2 * count]
    at = 2 * count + 1
    if last:
        sq_in = refs[at + HALVES]
        at += HALVES + 1
    k = refs[at : at + HALVES]
    extra, lhs, inv, buf, sems, csum = refs[at + HALVES :]
    z, core = position(fast)
    half = k[0].shape[1]
    rows_all = k[0].shape[0]

    def copies(h):
        return [
            pltpu.make_async_copy(
                unit.at[lax.bitwise_xor(z, s) if fast else s, pl.ds(h * half, half), :],
                buf.at[h % 2, n],
                sems.at[h % 2, n],
            )
            for n, s in enumerate(slots)
        ]

    for h in range(2):
        for c in copies(h):
            c.start()
    for n in range(count):
        a, b = own[n][...], sib[n][...]
        first, second = order(fast, core, a, b)
        width = a.shape[1]
        lhs[n, :, :width] = first
        lhs[n, :, width:] = second
    step = min(64, rows_all)

    def squares(t, c):
        rows = pl.ds(pl.multiple_of(t * step, step), step)
        sq = sq_in[rows, :] if last else jnp.zeros((step, LANES), F32)
        for n in range(count):
            for l in range(lhs.shape[2] // LANES):
                sq = sq + square(lhs[n, rows, l * LANES : (l + 1) * LANES])
        if last:
            total = jnp.sum(sq, axis=1, keepdims=True)
            inv[rows, :] = jnp.broadcast_to(lax.rsqrt(total + NORM_EPS) * scale, (step, LANES))
        else:
            extra[rows, :] = sq
        return c

    lax.fori_loop(0, rows_all // step, squares, 0, unroll=2)
    if last:
        csum[...] = jnp.zeros(csum.shape, F32)
    for h in range(HALVES):
        for c in copies(h):
            c.wait()

        def body(t, carry, h=h):
            rows = pl.ds(pl.multiple_of(t * block, block), block)
            for n in range(half // tile):
                d = None
                for i in range(count):
                    p = lax.dot_general(
                        lhs[i, rows, :],
                        buf[h % 2, i, n * tile : (n + 1) * tile, :],
                        (((1,), (1,)), ((), ())),
                        preferred_element_type=F32,
                    )
                    d = p if d is None else d + p
                for l in range(tile // LANES):
                    cols = slice(n * tile + l * LANES, n * tile + (l + 1) * LANES)
                    x = d[:, l * LANES : (l + 1) * LANES]
                    if last:
                        x = jnp.exp2((x + k[h][rows, cols]) * inv[rows, :])
                        full = slice(h * half + cols.start, h * half + cols.stop)
                        csum[:, full] += jnp.sum(x.reshape(block // 8, 8, LANES), axis=0)
                    k[h][rows, cols] = x
            return carry

        lax.fori_loop(0, rows_all // block, body, 0)
        if h + 2 < HALVES:
            for c in copies(h + 2):
                c.start()
    if last:
        extra[...] = jnp.sum(csum[...], axis=0, keepdims=True)


def tree(terms):
    while len(terms) > 1:
        paired = [terms[i] + terms[i + 1] for i in range(0, len(terms) - 1, 2)]
        terms = paired + ([terms[-1]] if len(terms) % 2 else [])
    return terms[0]


def col_scale(cs, scale, c_ref):
    total = cs[0][...]
    for p in cs[1:]:
        total = total + p[...]
    if total.shape[0] > 1:
        total = jnp.sum(total, axis=0, keepdims=True)
    c_ref[...] = 1.0 / (scale * total)


def spread(c_ref, start, count):
    return [
        jnp.broadcast_to(c_ref[:, start + i * LANES : start + (i + 1) * LANES], (8, LANES)) for i in range(count)
    ]


def row_pass_kernel(parts, scale, *refs):
    cs = refs[:parts]
    k = refs[parts : parts + HALVES]
    out, c_ref, acc = refs[parts + HALVES :]
    col_scale(cs, scale, c_ref)
    rows_all, half = k[0].shape
    block = min(128, rows_all)
    count = half // LANES
    for h in range(HALVES):
        cb = spread(c_ref, h * half, count)

        def inner(t, carry, h=h, cb=cb):
            for u in range(block // 8):
                rows = pl.ds(pl.multiple_of(t * block + u * 8, 8), 8)
                x = k[h][rows, :]
                s = tree([x[:, i * LANES : (i + 1) * LANES] * cb[i] for i in range(count)])
                acc[rows, :] = acc[rows, :] + s if h else s
            return carry

        lax.fori_loop(0, rows_all // block, inner, 0)
    out[...] = rows_to_lanes(acc[...])


def col_pass_kernel(parts, scale, *refs):
    rs = refs[:parts]
    k = refs[parts : parts + HALVES]
    out, rb = refs[parts + HALVES :]
    total = rs[0][...]
    for p in rs[1:]:
        total = total + p[...]
    lanes_to_rows(1.0 / (scale * total), rb)
    rows_all, half = k[0].shape
    block = min(64, rows_all)
    count = half // LANES
    for h in range(HALVES):

        def inner(t, accs, h=h):
            accs = list(accs)
            for u in range(block // 8):
                rows = pl.ds(pl.multiple_of(t * block + u * 8, 8), 8)
                x = k[h][rows, :]
                r = rb[rows, :]
                for i in range(count):
                    accs[i] = accs[i] + x[:, i * LANES : (i + 1) * LANES] * r
            return tuple(accs)

        accs = lax.fori_loop(0, rows_all // block, inner, tuple(jnp.zeros((8, LANES), F32) for _ in range(count)))
        for i in range(count):
            at = h * half + i * LANES
            out[:, at : at + LANES] = jnp.sum(accs[i], axis=0, keepdims=True)


def last_pass_kernel(parts, scale, *refs):
    cs = refs[:parts]
    k = refs[parts : parts + HALVES]
    q = refs[parts + HALVES : parts + HALVES + PIECES]
    tot, out, c_ref, acc, cross, buf, sems = refs[parts + HALVES + PIECES :]
    depth = buf.shape[0]
    copy = lambda j: pltpu.make_async_copy(q[j], buf.at[j % depth], sems.at[j % depth])
    for j in range(depth):
        copy(j).start()
    col_scale(cs, scale, c_ref)
    rows_all, _ = k[0].shape
    piece = q[0].shape[1]
    per_half = PIECES // HALVES
    block = min(64, rows_all)
    count = piece // LANES
    for j in range(PIECES):
        h, base = j // per_half, (j % per_half) * piece
        cb = spread(c_ref, j * piece, count)
        copy(j).wait()

        def inner(t, carry, j=j, h=h, base=base, cb=cb):
            for u in range(block // 16):
                both = pl.ds(pl.multiple_of(t * block + u * 16, 16), 16)
                logit = buf[j % depth, both, :].astype(jnp.int32).astype(F32)
                for v in range(2):
                    rows = pl.ds(pl.multiple_of(t * block + u * 16 + v * 8, 8), 8)
                    x = k[h][rows, base : base + piece]
                    a = [x[:, i * LANES : (i + 1) * LANES] * cb[i] for i in range(count)]
                    w = [a[i] * logit[v * 8 : v * 8 + 8, i * LANES : (i + 1) * LANES] for i in range(count)]
                    s, w = tree(a), tree(w)
                    acc[rows, :] = acc[rows, :] + s if j else s
                    cross[rows, :] = cross[rows, :] + w if j else w
            return carry

        lax.fori_loop(0, rows_all // block, inner, 0)
        if j + depth < PIECES:
            copy(j + depth).start()
    blocks = rows_all // LANES
    out[:blocks, :] = rows_to_lanes(acc[...])
    out[blocks : 2 * blocks, :] = rows_to_lanes(tot[...])
    out[2 * blocks :, :] = rows_to_lanes(cross[...]) * (1.0 / (LOGIT_STEPS * LOG2E))


def piece_copies(fast, z, offset, unit, buf, sems):
    piece = buf.shape[1]
    return [
        pltpu.make_async_copy(
            unit.at[lax.bitwise_xor(z, s) if fast else s, pl.ds(offset, piece), :], buf.at[s], sems.at[s]
        )
        for s in range(CHUNKS)
    ]


def prep_kernel(fast, scale, *refs):
    own = refs[:CHUNKS]
    sib = refs[CHUNKS : 2 * CHUNKS]
    unit, lhs, inv, ahead, sems = refs[2 * CHUNKS :]
    z, core = position(fast)
    copies = piece_copies(fast, z, 0, unit, ahead, sems)
    for c in copies:
        c.start()
    width = own[0].shape[1]
    sq = jnp.zeros(inv.shape, F32)
    for s in range(CHUNKS):
        a, b = own[s][...], sib[s][...]
        first, second = order(fast, core, a, b)
        lhs[s, :, :width] = first
        lhs[s, :, width:] = second
        sq = sq + square(a) + square(b)
    total = jnp.sum(sq, axis=1, keepdims=True)
    inv[...] = jnp.broadcast_to(lax.rsqrt(total + NORM_EPS) * scale, inv.shape)
    for c in copies:
        c.wait()


def logit_kernel(fast, offset, tile, block, *refs):
    lhs, inv, buf = refs[:3]
    if offset is None:
        tot_in, tot_out, q_ref, qbuf, qsems = refs[3:]
        copies = []
    else:
        unit, tot_in, tot_out, q_ref, ahead, qbuf, qsems, sems = refs[3:]
        copies = piece_copies(fast, position(fast)[0], offset, unit, ahead, sems)
    rows_all, piece = q_ref.shape
    steps = piece // tile

    def store(t):
        rows = pl.ds(pl.multiple_of(t * block, block), block)
        return pltpu.make_async_copy(qbuf.at[rows, :], q_ref.at[rows, :], qsems.at[t])

    for c in copies:
        c.start()

    def body(t, carry):
        rows = pl.ds(pl.multiple_of(t * block, block), block)
        for n in range(steps):
            d = None
            for s in range(CHUNKS):
                part = lax.dot_general(
                    lhs[s, rows, :],
                    buf[s, n * tile : (n + 1) * tile, :],
                    (((1,), (1,)), ((), ())),
                    preferred_element_type=F32,
                )
                d = part if d is None else d + part
            sums = []
            for l in range(tile // LANES):
                logit = d[:, l * LANES : (l + 1) * LANES] * inv[rows, :]
                sums.append(jnp.exp2(logit))
                q = jnp.round(logit * LOGIT_STEPS).astype(jnp.int32).astype(jnp.int16)
                qbuf[rows, n * tile + l * LANES : n * tile + (l + 1) * LANES] = q
            before = tot_out if n else tot_in
            tot_out[rows, :] = before[rows, :] + tree(sums)
        store(t).start()
        return carry

    lax.fori_loop(0, rows_all // block, body, 0)
    for t in range(rows_all // block):
        store(t).wait()
    for c in copies:
        c.wait()


def write_kernel(parts, scale, tile, *refs):
    rs = refs[:parts]
    k = refs[parts : parts + HALVES]
    c_ref = refs[parts + HALVES]
    out, rb, buf, sems = refs[parts + HALVES + 1 :]
    blocks = rb.shape[0] // LANES
    total = rs[0][:blocks, :]
    for p in rs[1:]:
        total = total + p[:blocks, :]
    lanes_to_rows(scale / total, rb)
    rows_all = k[0].shape[0]
    half = k[0].shape[1]
    depth = buf.shape[0]
    steps = rows_all // tile

    def copy(i, slot):
        return pltpu.make_async_copy(
            buf.at[slot], out.at[pl.ds(pl.multiple_of(i * tile, tile), tile), :], sems.at[slot]
        )

    def step(i, carry):
        slot = lax.rem(i, depth)

        @pl.when(i >= depth)
        def _():
            copy(i - depth, slot).wait()

        rows = pl.ds(pl.multiple_of(i * tile, tile), tile)
        r = rb[rows, :]
        for h in range(HALVES):
            for n in range(half // LANES):
                oc = slice(h * half + n * LANES, h * half + (n + 1) * LANES)
                x = k[h][rows, n * LANES : (n + 1) * LANES]
                buf[slot, :, oc] = (x * c_ref[:, oc] * r).astype(BF16)
        copy(i, slot).start()
        return carry

    lax.fori_loop(0, steps, step, 0)
    for i in range(max(steps - depth, 0), steps):
        copy(i, i % depth).wait()


def swap(x, axis, distance):
    n = lax.axis_size(axis)
    return lax.ppermute(x, axis, [(i, i ^ distance) for i in range(n)])


def radices(n):
    out = []
    while n % 4 == 0:
        out.append(4)
        n //= 4
    if n > 1:
        out.insert(0, n)
    return out


def reduce_parts(x, axis, steps):
    stride = 1
    parts = [x]
    for radix in steps:
        if len(parts) > 1:
            x = functools.reduce(lambda a, b: a + b, parts)
        parts = [x] + [swap(x, axis, stride * d) for d in range(1, radix)]
        stride *= radix
    return parts


def first_slices(x):
    near = swap(x, "proto", 2)
    far = swap(x, "proto", 4)
    last = swap(far, "proto", 2)
    own = [x, near, far, last]
    return own, [swap(v, "proto", 1) for v in own]


def second_slices(x, gate):
    far = [swap(x, "proto", 2 * s) for s in range(1, CHUNKS)]
    *far, gate = lax.optimization_barrier((*far, gate))
    own = [x, *far]
    return own, [swap(v, "proto", 1) for v in own], gate


def slices_plain(x, width):
    full = lax.all_gather(x, "proto", axis=1, tiled=True)
    parts = [full[:, i * width : (i + 1) * width] for i in range(2 * CHUNKS)]
    return parts[0::2], parts[1::2]


def local(view_codes, predictor_view_embeddings, prototypes):
    nb, npr = lax.axis_size("batch"), lax.axis_size("proto")
    rows = view_codes.shape[0]
    cols, dim = prototypes.shape
    half = cols // HALVES
    width = dim // CHUNKS
    piece = cols // PIECES
    rows_total, protos_total = rows * nb, cols * npr
    fast = npr == NEAR and view_codes.shape[1] * 2 == width
    sds = jax.ShapeDtypeStruct
    vec = sds((1, cols), F32)
    packed = sds((rows // LANES, LANES), F32)

    ntile = min(512, half)
    unit = call(
        functools.partial(norm_kernel, ntile, 4),
        pltpu.HBM((CHUNKS, cols, width), BF16),
        [HB],
        (prototypes,),
        scratch=[
            pltpu.VMEM((4, ntile, dim), BF16),
            pltpu.VMEM((4, CHUNKS, ntile, width), BF16),
            pltpu.VMEM((ntile, LANES), F32),
            pltpu.SemaphoreType.DMA((4,)),
            pltpu.SemaphoreType.DMA((4,)),
        ],
        limit=14,
        flops=5e9,
    )
    if fast:
        own1, sib1 = first_slices(view_codes)
    else:
        own1, sib1 = slices_plain(view_codes, width // 2)

    block = min(512, rows)
    tile = min(256, piece)
    kshape = tuple(pltpu.VMEM((rows, half), F32) for _ in range(HALVES))
    k, extra = (), ()
    per_stage = CHUNKS // 2
    for s in range(2):
        last = s == 1
        slots = tuple(range(s * per_stage, (s + 1) * per_stage))
        nin = 2 * per_stage + 1
        res = call(
            functools.partial(stage_kernel, fast, slots, last, LOG2E / EPSILON, tile, block),
            kshape + (vec if last else sds((rows, LANES), F32),),
            [VM] * (nin - 1) + [HB] + [VM] * (HALVES + 1 if last else 0),
            (*[own1[i] for i in slots], *[sib1[i] for i in slots], unit, *k, *extra),
            scratch=[
                pltpu.VMEM((per_stage, rows, width), BF16),
                pltpu.VMEM((rows, LANES), F32),
                pltpu.VMEM((2, per_stage, half, width), BF16),
                pltpu.SemaphoreType.DMA((2, per_stage)),
                pltpu.VMEM((8, cols), F32),
            ],
            limit=8,
            alias={nin + h: h for h in range(HALVES)} if last else None,
            flops=2 * rows * cols * width * per_stage,
        )
        k, extra = res[:HALVES], res[HALVES:]
    col_part = extra[0]
    if fast:
        own2, sib2, col_part = second_slices(predictor_view_embeddings, col_part)
    else:
        own2, sib2 = slices_plain(predictor_view_embeddings, width // 2)

    ahead_shape = sds((CHUNKS, piece, width), BF16)
    lhs2, inv2, ahead = call(
        functools.partial(prep_kernel, fast, LOG2E / SOFTMAX_TEMP_VALUE),
        (sds((CHUNKS, rows, width), BF16), sds((rows, LANES), F32), ahead_shape),
        [VM] * (2 * CHUNKS) + [HB],
        (*own2, *sib2, unit),
        scratch=[pltpu.SemaphoreType.DMA((CHUNKS,))],
        flops=5e8,
    )
    tot = jnp.zeros((rows, LANES), F32)
    quant = []

    def logits(tot, ahead, after):
        j = len(quant)
        more = j + 1 < PIECES
        tot, after = lax.optimization_barrier((tot, after))
        tot, q, *rest = call(
            functools.partial(logit_kernel, fast, (j + 1) * piece if more else None, tile, block),
            (sds((rows, LANES), F32), pltpu.HBM((rows, piece), jnp.int16)) + ((ahead_shape,) if more else ()),
            [VM] * 3 + ([HB] if more else []) + [VM],
            (lhs2, inv2, ahead) + ((unit,) if more else ()) + (tot,),
            scratch=[pltpu.VMEM((rows, piece), jnp.int16), pltpu.SemaphoreType.DMA((rows // block,))]
            + ([pltpu.SemaphoreType.DMA((CHUNKS,))] if more else []),
            limit=6,
            flops=2 * rows * piece * dim,
        )
        quant.append(q)
        return tot, (rest[0] if more else None)

    def cover(parts, tot, ahead, count):
        for _ in range(min(count, PIECES - len(quant))):
            tot, ahead = logits(tot, ahead, parts[0])
        *head, tail = parts
        tail, tot = lax.optimization_barrier((tail, tot))
        return [*head, tail], tot, ahead

    for it in range(SINK_ITERS):
        cparts = reduce_parts(col_part, "batch", radices(nb))
        cparts, tot, ahead = cover(cparts, tot, ahead, COVER[2 * it])
        if it < SINK_ITERS - 1:
            row_part, _ = call(
                functools.partial(row_pass_kernel, len(cparts), float(protos_total)),
                (packed, vec),
                [VM] * (len(cparts) + HALVES),
                (*cparts, *k),
                scratch=[pltpu.VMEM((rows, LANES), F32)],
                flops=4e9,
            )
            rparts = reduce_parts(row_part, "proto", radices(npr))
            rparts, tot, ahead = cover(rparts, tot, ahead, COVER[2 * it + 1])
            col_part = call(
                functools.partial(col_pass_kernel, len(rparts), float(rows_total)),
                vec,
                [VM] * (len(rparts) + HALVES),
                (*rparts, *k),
                scratch=[pltpu.VMEM((rows, LANES), F32)],
                flops=4e9,
            )

    blocks = rows // LANES
    both, c = call(
        functools.partial(last_pass_kernel, len(cparts), float(protos_total)),
        (sds((3 * blocks, LANES), F32), vec),
        [VM] * (len(cparts) + HALVES) + [HB] * PIECES + [VM],
        (*cparts, *k, *quant, tot),
        scratch=[
            pltpu.VMEM((rows, LANES), F32),
            pltpu.VMEM((rows, LANES), F32),
            pltpu.VMEM((4, rows, piece), jnp.int16),
            pltpu.SemaphoreType.DMA((4,)),
        ],
        limit=12,
        flops=8e9,
    )
    bparts = reduce_parts(both, "proto", radices(npr))
    otile = 64
    assignments = call(
        functools.partial(write_kernel, len(bparts), float(protos_total), otile),
        pltpu.HBM((rows, cols), BF16),
        [VM] * (len(bparts) + HALVES + 1),
        (*bparts, *k, c),
        scratch=[
            pltpu.VMEM((rows, LANES), F32),
            pltpu.VMEM((3, otile, cols), BF16),
            pltpu.SemaphoreType.DMA((3,)),
        ],
        flops=4e9,
    )
    sums = functools.reduce(lambda a, b: a + b, bparts)
    loss = jnp.log(sums[blocks : 2 * blocks]) - sums[2 * blocks :] / sums[:blocks]
    return assignments, loss.reshape(rows)


def solution(mesh):
    placed = (P("batch", "proto"), P("batch", "proto"), P("proto", None))

    return jax.shard_map(
        local,
        mesh=mesh,
        in_specs=placed,
        out_specs=(P("batch", "proto"), P("batch")),
        check_vma=False,
    )
```

time: 419 us -> 154 us (0.37); the launches traced: 412 us -> 154 us
  matrix products: 216 us -> 0 us
  blocking collectives: 117 us -> 0 us
  Pallas kernels: 0 us -> 98.6 us
  starting transfers between devices: 3.45 us -> 34.2 us
  waiting for transfers between devices: 48.9 us -> 19.6 us
  between operations: 14.6 us -> 1.14 us
  other arithmetic: 12.2 us -> 0.62 us
    dot_general x8 -> x0, matrix products: 216 us -> none  [the longest x3 95.2 us: local(): row_part = jnp.dot(kernel, scale_cols, precision=lax.Precision.HIGHEST)]
    psum x7 -> x0, blocking collectives: 101 us -> none  [the longest x3 45.9 us: local(): col_sums = lax.psum(col_part, 'batch')]
    pallas_call x0 -> x18, Pallas kernels: none -> 98.6 us  [call(): pl.pallas_call(kernel, out_shape=outs, in_specs=ins, out_specs=jax.tree.m...]
    all_gather x1 -> x0, waiting for transfers between devices: 39.5 us -> none  [local(): piece = lax.all_gather(stacked, 'proto', axis=1, tiled=True)]
    ppermute x0 -> x35, starting transfers between devices: none -> 34.2 us  [swap(): return lax.ppermute(x, axis, [(i, i ^ distance) for i in range(n)])]
    ppermute x0 -> x35, waiting for transfers between devices: none -> 19.6 us  [swap(): return lax.ppermute(x, axis, [(i, i ^ distance) for i in range(n)])]
    all_to_all x1 -> x0, blocking collectives: 16.1 us -> none  [local(): lax.all_to_all(view_codes, 'proto', split_axis=0, concat_axis=1, tiled=True)]
    reduce_sum x2 -> x0, other arithmetic: 10.7 us -> none  [the longest x1 7.37 us: normalized(): jnp.sum(weights * weights, axis=1, keepdims=True) + 1e-06]
  transfers between devices with their start and end apart: 2 -> 35, of which waited for: 2 -> 7; matrix products, arithmetic and copies ran while one was open for 2% -> 0% of each run, Pallas kernels for 0% -> 45%
where the time goes in v1:
time: 154 us
  Pallas kernels  98.6 us (64%)
  starting transfers between devices  34.2 us (22%)
  waiting for transfers between devices  19.6 us (13%)
    pallas_call x18, Pallas kernels, call(): pl.pallas_call(kernel, out_shape=outs, in_specs=ins, out_specs=jax.tree.m...  98.6 us
    ppermute x35, starting transfers between devices, swap(): return lax.ppermute(x, axis, [(i, i ^ distance) for i in range(n)])  34.2 us
    ppermute x35, waiting for transfers between devices, swap(): return lax.ppermute(x, axis, [(i, i ^ distance) for i in range(n)])  19.6 us
  transfers between devices with their start and end apart: 35, of which 7 were waited for; matrix products, arithmetic and copies ran while one was open for 0% of the time, Pallas kernels for 45%

profile of v1, /device:TPU:0, one launch (start us, length us, event | category | flops | bytes accessed | tf_op | source)
XLA Modules:
  0.0 154.2 jit_solution(13342385879833992277)
XLA Ops:
  0.6 3.1 %collective-permute-start.7 = (bf16[1024,128]{1,0:T(8,128)(2,1)}, bf16[1024,128]{1,0:T(8,128)(2,1)S(1)}, u32[]{:S(2)}, u32[]{:S(2)}) collective-permute-start(bf16[1024,128]{1,0:T(8,128)(2,1)} %refs_0_.2), channel_id=1, source_target_pairs={{0,2},{1,3},{2,0},{3,1},{4,6},{5,7},{6,4},{7,5},{8,10},{9,11},{10,... | collective-permute-start | bytes 786440 | tf_op jit(solution)/shard_map/ppermute | solution.py:467
  3.8 2.6 %collective-permute-start.3 = (bf16[1024,128]{1,0:T(8,128)(2,1)}, bf16[1024,128]{1,0:T(8,128)(2,1)S(1)}, u32[]{:S(2)}, u32[]{:S(2)}) collective-permute-start(bf16[1024,128]{1,0:T(8,128)(2,1)} %refs_0_.2), channel_id=1, source_target_pairs={{0,4},{1,5},{2,6},{3,7},{4,0},{5,1},{6,2},{7,3},{8,12},{9,13},{10,... | collective-permute-start | bytes 786440 | tf_op jit(solution)/shard_map/ppermute | solution.py:467
  6.4 0.0 collective-permute-start.8
  6.4 0.4 collective-permute-start
  6.8 0.0 collective-permute-start.1
  6.8 9.8 %collective-permute-done.7.refs_1_ = bf16[1024,128]{1,0:T(8,128)(2,1)S(1)} collective-permute-done((bf16[1024,128]{1,0:T(8,128)(2,1)}, bf16[1024,128]{1,0:T(8,128)(2,1)S(1)}, u32[]{:S(2)}, u32[]{:S(2)}) %collective-permute-start.7) | collective-permute-done | bytes 262176 | tf_op jit(solution)/shard_map/ppermute | solution.py:467
  16.6 3.2 %collective-permute-done.3.refs_0_ = bf16[1024,128]{1,0:T(8,128)(2,1)S(1)} collective-permute-done((bf16[1024,128]{1,0:T(8,128)(2,1)}, bf16[1024,128]{1,0:T(8,128)(2,1)S(1)}, u32[]{:S(2)}, u32[]{:S(2)}) %collective-permute-start.3) | collective-permute-done | bytes 262176 | tf_op jit(solution)/shard_map/ppermute | solution.py:467
  19.8 0.1 collective-permute-start.4
  19.8 12.9 %shard_map.50.refs_4_.refs_8_.refs_3_ = bf16[4,8192,256]{2,1,0:T(8,128)(2,1)} custom-call(bf16[8192,1024]{1,0:T(8,128)(2,1)} %p_ref.1), custom_call_target="tpu_custom_call" | custom-call | flops 5000000000 | tf_op jit(solution)/shard_map/pallas_call | solution.py:36
  32.8 0.0 collective-permute-done.8.refs_2_
  32.8 2.5 %collective-permute-start.2 = (bf16[1024,128]{1,0:T(8,128)(2,1)S(1)}, bf16[1024,128]{1,0:T(8,128)(2,1)S(1)}, u32[]{:S(2)}, u32[]{:S(2)}) collective-permute-start(bf16[1024,128]{1,0:T(8,128)(2,1)S(1)} %copy-done), channel_id=1, source_target_pairs={{0,6},{1,7},{2,4},{3,5},{4,2},{5,3},{6,0},{7,1},{8,14},{9,15},{10,... | collective-permute-start | bytes 786440 | tf_op jit(solution)/shard_map/ppermute | solution.py:467
  35.3 0.0 collective-permute-done.9.refs_3_
  35.3 0.0 collective-permute-start.5
  35.3 0.5 collective-permute-start.6
  35.8 11.9 %shard_map.51 = (f32[1024,2048]{1,0:T(8,128)S(1)}, f32[1024,2048]{1,0:T(8,128)S(1)}, f32[1024,2048]{1,0:T(8,128)S(1)}, f32[1024,2048]{1,0:T(8,128)S(1)}, f32[1024,128]{1,0:T(8,128)S(1)}) custom-call(bf16[1024,128]{1,0:T(8,128)(2,1)S(1)} %copy-done.1, bf16[1024,128]{1,0:T(8,128)(2,1)S(1)} %collective-permute-done.7.refs_1_, ...), custom_call_target="tpu_custom_call" | custom-call | flops 8589934592 | tf_op jit(solution)/shard_map/pallas_call | solution.py:36
  47.7 0.1 collective-permute-start.13
  47.9 12.4 %shard_map.52 = (f32[1024,2048]{1,0:T(8,128)S(1)}, f32[1024,2048]{1,0:T(8,128)S(1)}, f32[1024,2048]{1,0:T(8,128)S(1)}, f32[1024,2048]{1,0:T(8,128)S(1)}, f32[1,8192]{1,0:T(1,128)S(1)}) custom-call(bf16[1024,128]{1,0:T(8,128)(2,1)S(1)} %collective-permute-done.3.refs_0_, ...), custom_call_target="tpu_custom_call", output_to_operand_aliasing={{0}: (5, {}), {1}: (6, {}), {2}: (7, {}), {3}: (8, {})} | custom-call | flops 8589934592 | tf_op jit(solution)/shard_map/pallas_call | solution.py:36
  60.2 0.0 collective-permute-done.refs_1_
  60.2 0.0 collective-permute-done.1.refs_2_
  60.3 0.5 collective-permute-start.14
  60.8 0.1 collective-permute-start.15
  60.8 0.4 collective-permute-start.16
  61.3 2.4 %collective-permute-start.12 = (f32[1,8192]{1,0:T(1,128)S(1)}, f32[1,8192]{1,0:T(1,128)S(1)}, u32[]{:S(2)}, u32[]{:S(2)}) collective-permute-start(f32[1,8192]{1,0:T(1,128)S(1)} %get-tuple-element.70.refs_0_), channel_id=1, source_target_pairs={{0,24},{8,16},{16,8},{24,0},{1,25},{9,17},{17,9},{25,1},{2,26},{10... | collective-permute-start | bytes 98312 | tf_op jit(solution)/shard_map/ppermute | solution.py:467
  63.7 0.0 collective-permute-done.13.refs_4_
  63.7 0.5 collective-permute-start.10
  64.3 0.0 collective-permute-done.14.refs_5_
  64.3 0.5 collective-permute-start.11
  64.8 0.0 collective-permute-done.15.refs_6_
  64.8 2.1 %shard_map.53 = (bf16[4,1024,256]{2,1,0:T(8,128)(2,1)S(1)}, f32[1024,128]{1,0:T(8,128)S(1)}, bf16[4,1024,256]{2,1,0:T(8,128)(2,1)S(1)}) custom-call(bf16[1024,128]{1,0:T(8,128)(2,1)S(1)} %copy-done, bf16[1024,128]{1,0:T(8,128)(2,1)S(1)} %collective-permute-done.refs_1_, bf16[1024,128]{1,0:T(8,128)(2,1)S(1)} %collective-permute-done.1.refs_2_, ...), custom_call_target="tpu_custom_call" | custom-call | flops 500000000 | tf_op jit(solution)/shard_map/pallas_call | solution.py:36
  66.9 3.8 %shard_map.54 = (f32[1024,128]{1,0:T(8,128)S(1)}, s16[1024,1024]{1,0:T(8,128)(2,1)}, bf16[4,1024,256]{2,1,0:T(8,128)(2,1)S(1)}) custom-call(bf16[4,1024,256]{2,1,0:T(8,128)(2,1)S(1)} %get-tuple-element.74.refs_0_, f32[1024,128]{1,0:T(8,128)S(1)} %get-tuple-element.75.refs_1_, bf16[4,1024,256]{2,1,0:T(8,128)(2,1)S(1)} %get-tuple-element.76.refs_2_, ...), custom_call_target="tpu_custom_call" | custom-call | flops 2147483648 | tf_op jit(solution)/shard_map/pallas_call | solution.py:36
  70.7 4.0 %shard_map.55 = (f32[1024,128]{1,0:T(8,128)S(1)}, s16[1024,1024]{1,0:T(8,128)(2,1)}, bf16[4,1024,256]{2,1,0:T(8,128)(2,1)S(1)}) custom-call(bf16[4,1024,256]{2,1,0:T(8,128)(2,1)S(1)} %get-tuple-element.74.refs_0_, f32[1024,128]{1,0:T(8,128)S(1)} %get-tuple-element.75.refs_1_, bf16[4,1024,256]{2,1,0:T(8,128)(2,1)S(1)} %get-tuple-element.78.refs_2_, ...), custom_call_target="tpu_custom_call" | custom-call | flops 2147483648 | tf_op jit(solution)/shard_map/pallas_call | solution.py:36
  74.8 0.0 collective-permute-done.10.refs_1_
  74.8 3.0 %shard_map.56 = (f32[8,128]{1,0:T(8,128)S(1)}, f32[1,8192]{1,0:T(1,128)}) custom-call(f32[1,8192]{1,0:T(1,128)S(1)} %get-tuple-element.70.refs_0_, f32[1,8192]{1,0:T(1,128)S(1)} %collective-permute-done.10.refs_1_, f32[1,8192]{1,0:T(1,128)S(1)} %collective-permute-done.11.refs_2_, f32[1,8192]{1,0:T(1,128)S(1)} %collective-permute-done.12.refs_3_, ...), custom_call_target="tpu_custom_call" | custom-call | flops 4000000000 | tf_op jit(solution)/shard_map/pallas_call | solution.py:36
  77.8 1.2 collective-permute-done.17
  78.9 1.4 collective-permute-start.20
  80.3 0.2 collective-permute-start.18
  80.5 2.8 %collective-permute-start.19 = (f32[8,128]{1,0:T(8,128)S(1)}, f32[8,128]{1,0:T(8,128)S(1)}, u32[]{:S(2)}, u32[]{:S(2)}) collective-permute-start(f32[8,128]{1,0:T(8,128)S(1)} %add.18.refs_0_), channel_id=1, source_target_pairs={{0,4},{1,5},{2,6},{3,7},{4,0},{5,1},{6,2},{7,3},{8,12},{9,13},{10,... | collective-permute-start | bytes 12296 | tf_op jit(solution)/shard_map/ppermute | solution.py:467
  83.3 3.8 %shard_map.57 = (f32[1024,128]{1,0:T(8,128)S(1)}, s16[1024,1024]{1,0:T(8,128)(2,1)}, bf16[4,1024,256]{2,1,0:T(8,128)(2,1)S(1)}) custom-call(bf16[4,1024,256]{2,1,0:T(8,128)(2,1)S(1)} %get-tuple-element.74.refs_0_, f32[1024,128]{1,0:T(8,128)S(1)} %get-tuple-element.75.refs_1_, bf16[4,1024,256]{2,1,0:T(8,128)(2,1)S(1)} %get-tuple-element.88.refs_2_, ...), custom_call_target="tpu_custom_call" | custom-call | flops 2147483648 | tf_op jit(solution)/shard_map/pallas_call | solution.py:36
  87.2 3.9 %shard_map.58 = (f32[1024,128]{1,0:T(8,128)S(1)}, s16[1024,1024]{1,0:T(8,128)(2,1)}, bf16[4,1024,256]{2,1,0:T(8,128)(2,1)S(1)}) custom-call(bf16[4,1024,256]{2,1,0:T(8,128)(2,1)S(1)} %get-tuple-element.74.refs_0_, f32[1024,128]{1,0:T(8,128)S(1)} %get-tuple-element.75.refs_1_, bf16[4,1024,256]{2,1,0:T(8,128)(2,1)S(1)} %get-tuple-element.91.refs_2_, ...), custom_call_target="tpu_custom_call" | custom-call | flops 2147483648 | tf_op jit(solution)/shard_map/pallas_call | solution.py:36
  91.1 2.8 %shard_map.59.refs_0_ = f32[1,8192]{1,0:T(1,128)S(1)} custom-call(f32[8,128]{1,0:T(8,128)S(1)} %add.18.refs_0_, f32[8,128]{1,0:T(8,128)S(1)} %collective-permute-done.18.refs_1_, f32[8,128]{1,0:T(8,128)S(1)} %collective-permute-done.19.refs_2_, f32[8,128]{1,0:T(8,128)S(1)} %collective-permute-done.20.refs_3_, f32[1024,2048]{1,0:T(8,128)S(1)} %get-tuple-element.83.refs_4_, ...), custom_call_target="tpu_custom_call" | custom-call | flops 4000000000 | tf_op jit(solution)/shard_map/pallas_call | solution.py:36
  93.9 2.5 %collective-permute-start.23 = (f32[1,8192]{1,0:T(1,128)S(1)}, f32[1,8192]{1,0:T(1,128)S(1)}, u32[]{:S(2)}, u32[]{:S(2)}) collective-permute-start(f32[1,8192]{1,0:T(1,128)S(1)} %shard_map.59.refs_0_), channel_id=1, source_target_pairs={{0,24},{8,16},{16,8},{24,0},{1,25},{9,17},{17,9},{25,1},{2,26},{10... | collective-permute-start | bytes 98312 | tf_op jit(solution)/shard_map/ppermute | solution.py:467
  96.4 0.5 collective-permute-start.21
  97.0 0.5 collective-permute-start.22
  97.5 3.8 %shard_map.60 = (f32[1024,128]{1,0:T(8,128)S(1)}, s16[1024,1024]{1,0:T(8,128)(2,1)}, bf16[4,1024,256]{2,1,0:T(8,128)(2,1)S(1)}) custom-call(bf16[4,1024,256]{2,1,0:T(8,128)(2,1)S(1)} %get-tuple-element.74.refs_0_, f32[1024,128]{1,0:T(8,128)S(1)} %get-tuple-element.75.refs_1_, bf16[4,1024,256]{2,1,0:T(8,128)(2,1)S(1)} %get-tuple-element.96.refs_2_, ...), custom_call_target="tpu_custom_call" | custom-call | flops 2147483648 | tf_op jit(solution)/shard_map/pallas_call | solution.py:36
  101.3 3.9 %shard_map.61 = (f32[1024,128]{1,0:T(8,128)S(1)}, s16[1024,1024]{1,0:T(8,128)(2,1)}, bf16[4,1024,256]{2,1,0:T(8,128)(2,1)S(1)}) custom-call(bf16[4,1024,256]{2,1,0:T(8,128)(2,1)S(1)} %get-tuple-element.74.refs_0_, f32[1024,128]{1,0:T(8,128)S(1)} %get-tuple-element.75.refs_1_, bf16[4,1024,256]{2,1,0:T(8,128)(2,1)S(1)} %get-tuple-element.99.refs_2_, ...), custom_call_target="tpu_custom_call" | custom-call | flops 2147483648 | tf_op jit(solution)/shard_map/pallas_call | solution.py:36
  105.2 3.0 %shard_map.62 = (f32[8,128]{1,0:T(8,128)S(1)}, f32[1,8192]{1,0:T(1,128)}) custom-call(f32[1,8192]{1,0:T(1,128)S(1)} %shard_map.59.refs_0_, f32[1,8192]{1,0:T(1,128)S(1)} %collective-permute-done.21.refs_1_, f32[1,8192]{1,0:T(1,128)S(1)} %collective-permute-done.22.refs_2_, f32[1,8192]{1,0:T(1,128)S(1)} %collective-permute-done.23.refs_3_, ...), custom_call_target="tpu_custom_call" | custom-call | flops 4000000000 | tf_op jit(solution)/shard_map/pallas_call | solution.py:36
  108.2 1.2 collective-permute-done.24
  109.4 1.4 collective-permute-start.27
  110.8 3.0 %collective-permute-start.26 = (f32[8,128]{1,0:T(8,128)S(1)}, f32[8,128]{1,0:T(8,128)S(1)}, u32[]{:S(2)}, u32[]{:S(2)}) collective-permute-start(f32[8,128]{1,0:T(8,128)S(1)} %add.19.refs_0_), channel_id=1, source_target_pairs={{0,4},{1,5},{2,6},{3,7},{4,0},{5,1},{6,2},{7,3},{8,12},{9,13},{10,... | collective-permute-start | bytes 12296 | tf_op jit(solution)/shard_map/ppermute | solution.py:467
  113.8 3.8 %shard_map.63 = (f32[1024,128]{1,0:T(8,128)S(1)}, s16[1024,1024]{1,0:T(8,128)(2,1)}, bf16[4,1024,256]{2,1,0:T(8,128)(2,1)S(1)}) custom-call(bf16[4,1024,256]{2,1,0:T(8,128)(2,1)S(1)} %get-tuple-element.74.refs_0_, f32[1024,128]{1,0:T(8,128)S(1)} %get-tuple-element.75.refs_1_, bf16[4,1024,256]{2,1,0:T(8,128)(2,1)S(1)} %get-tuple-element.105.refs_2_, ...), custom_call_target="tpu_custom_call" | custom-call | flops 2147483648 | tf_op jit(solution)/shard_map/pallas_call | solution.py:36
  117.6 2.8 %shard_map.64.refs_0_ = f32[1,8192]{1,0:T(1,128)S(1)} custom-call(f32[8,128]{1,0:T(8,128)S(1)} %add.19.refs_0_, f32[8,128]{1,0:T(8,128)S(1)} %collective-permute-done.25.refs_1_, f32[8,128]{1,0:T(8,128)S(1)} %collective-permute-done.26.refs_2_, f32[8,128]{1,0:T(8,128)S(1)} %collective-permute-done.27.refs_3_, f32[1024,2048]{1,0:T(8,128)S(1)} %get-tuple-element.83.refs_4_, ...), custom_call_target="tpu_custom_call" | custom-call | flops 4000000000 | tf_op jit(solution)/shard_map/pallas_call | solution.py:36
  120.4 2.5 %collective-permute-start.30 = (f32[1,8192]{1,0:T(1,128)S(1)}, f32[1,8192]{1,0:T(1,128)S(1)}, u32[]{:S(2)}, u32[]{:S(2)}) collective-permute-start(f32[1,8192]{1,0:T(1,128)S(1)} %shard_map.64.refs_0_), channel_id=1, source_target_pairs={{0,24},{8,16},{16,8},{24,0},{1,25},{9,17},{17,9},{25,1},{2,26},{10... | collective-permute-start | bytes 98312 | tf_op jit(solution)/shard_map/ppermute | solution.py:467
  122.9 0.5 collective-permute-start.28
  123.5 0.5 collective-permute-start.29
  124.0 3.8 %shard_map.65 = (f32[1024,128]{1,0:T(8,128)S(1)}, s16[1024,1024]{1,0:T(8,128)(2,1)}) custom-call(bf16[4,1024,256]{2,1,0:T(8,128)(2,1)S(1)} %get-tuple-element.74.refs_0_, f32[1024,128]{1,0:T(8,128)S(1)} %get-tuple-element.75.refs_1_, bf16[4,1024,256]{2,1,0:T(8,128)(2,1)S(1)} %get-tuple-element.110.refs_2_, f32[1024,128]{1,0:T(8,128)S(1)} %get-tuple-element.112.refs_3_), custom_call_target="tpu_custom_call" | custom-call | flops 2147483648 | tf_op jit(solution)/shard_map/pallas_call | solution.py:36
  127.8 9.5 %shard_map.66 = (f32[24,128]{1,0:T(8,128)S(1)}, f32[1,8192]{1,0:T(1,128)S(1)}) custom-call(f32[1,8192]{1,0:T(1,128)S(1)} %shard_map.64.refs_0_, f32[1,8192]{1,0:T(1,128)S(1)} %collective-permute-done.28.refs_1_, f32[1,8192]{1,0:T(1,128)S(1)} %collective-permute-done.29.refs_2_, f32[1,8192]{1,0:T(1,128)S(1)} %collective-permute-done.30.refs_3_, ...), custom_call_target="tpu_custom_call" | custom-call | flops 8000000000 | tf_op jit(solution)/shard_map/pallas_call | solution.py:36
  137.2 0.1 collective-permute-start.31
  137.3 1.2 collective-permute-done.31
  138.5 2.0 %collective-permute-start.33 = (f32[24,128]{1,0:T(8,128)S(1)}, f32[24,128]{1,0:T(8,128)S(1)}, u32[]{:S(2)}, u32[]{:S(2)}) collective-permute-start(f32[24,128]{1,0:T(8,128)S(1)} %add.20.refs_0_), channel_id=1, source_target_pairs={{0,4},{1,5},{2,6},{3,7},{4,0},{5,1},{6,2},{7,3},{8,12},{9,13},{10,... | collective-permute-start | bytes 36872 | tf_op jit(solution)/shard_map/ppermute | solution.py:467
  140.5 2.4 %collective-permute-start.34 = (f32[24,128]{1,0:T(8,128)S(1)}, f32[24,128]{1,0:T(8,128)S(1)}, u32[]{:S(2)}, u32[]{:S(2)}) collective-permute-start(f32[24,128]{1,0:T(8,128)S(1)} %add.20.refs_0_), channel_id=1, source_target_pairs={{0,6},{1,7},{2,4},{3,5},{4,2},{5,3},{6,0},{7,1},{8,14},{9,15},{10,... | collective-permute-start | bytes 36872 | tf_op jit(solution)/shard_map/ppermute | solution.py:467
  142.9 0.2 collective-permute-done.33.refs_2_
  143.1 2.8 %collective-permute-done.34.refs_3_ = f32[24,128]{1,0:T(8,128)S(1)} collective-permute-done((f32[24,128]{1,0:T(8,128)S(1)}, f32[24,128]{1,0:T(8,128)S(1)}, u32[]{:S(2)}, u32[]{:S(2)}) %collective-permute-start.34) | collective-permute-done | bytes 12320 | tf_op jit(solution)/shard_map/ppermute | solution.py:467
  146.0 0.6 fusion.1
  146.6 7.5 %shard_map.67 = bf16[1024,8192]{1,0:T(8,128)(2,1)} custom-call(f32[24,128]{1,0:T(8,128)S(1)} %add.20.refs_0_, f32[24,128]{1,0:T(8,128)S(1)} %collective-permute-done.32.refs_1_, f32[24,128]{1,0:T(8,128)S(1)} %collective-permute-done.33.refs_2_, f32[24,128]{1,0:T(8,128)S(1)} %collective-permute-done.34.refs_3_, f32[1024,2048]{1,0:T(8,128)S(1)} %get-tuple-element.83.refs_4_, ...), custom_call_target="tpu_custom_call" | custom-call | flops 4000000000 | tf_op jit(solution)/shard_map/pallas_call | solution.py:36
  (34 shorter events, 0.1 us)
Async XLA Ops:
  0.6 35.2 %copy-start.1 = (bf16[1024,128]{1,0:T(8,128)(2,1)S(1)}, bf16[1024,128]{1,0:T(8,128)(2,1)}, u32[]{:S(2)}) copy-start(bf16[1024,128]{1,0:T(8,128)(2,1)} %refs_0_.2) | copy-start | bytes 786436
  0.6 32.2 %copy-start = (bf16[1024,128]{1,0:T(8,128)(2,1)S(1)}, bf16[1024,128]{1,0:T(8,128)(2,1)}, u32[]{:S(2)}) copy-start(bf16[1024,128]{1,0:T(8,128)(2,1)} %refs_0_.3) | copy-start | bytes 786436
  0.6 16.0 %collective-permute-start.7 = (bf16[1024,128]{1,0:T(8,128)(2,1)}, bf16[1024,128]{1,0:T(8,128)(2,1)S(1)}, u32[]{:S(2)}, u32[]{:S(2)}) collective-permute-start(bf16[1024,128]{1,0:T(8,128)(2,1)} %refs_0_.2), channel_id=1, source_target_pairs={{0,2},{1,3},{2,0},{3,1},{4,6},{5,7},{6,4},{7,5},{8,10},{9,11},{10,... | collective-permute-start | bytes 786440 | tf_op jit(solution)/shard_map/ppermute | solution.py:467
  3.8 16.0 %collective-permute-start.3 = (bf16[1024,128]{1,0:T(8,128)(2,1)}, bf16[1024,128]{1,0:T(8,128)(2,1)S(1)}, u32[]{:S(2)}, u32[]{:S(2)}) collective-permute-start(bf16[1024,128]{1,0:T(8,128)(2,1)} %refs_0_.2), channel_id=1, source_target_pairs={{0,4},{1,5},{2,6},{3,7},{4,0},{5,1},{6,2},{7,3},{8,12},{9,13},{10,... | collective-permute-start | bytes 786440 | tf_op jit(solution)/shard_map/ppermute | solution.py:467
  6.4 26.4 %collective-permute-start.8 = (bf16[1024,128]{1,0:T(8,128)(2,1)}, bf16[1024,128]{1,0:T(8,128)(2,1)S(1)}, u32[]{:S(2)}, u32[]{:S(2)}) collective-permute-start(bf16[1024,128]{1,0:T(8,128)(2,1)} %refs_0_.2), channel_id=1, source_target_pairs={{0,1},{1,0},{2,3},{3,2},{4,5},{5,4},{6,7},{7,6},{8,9},{9,8},{10,11... | collective-permute-start | bytes 786440 | tf_op jit(solution)/shard_map/ppermute | solution.py:467
  6.4 53.9 %collective-permute-start = (bf16[1024,128]{1,0:T(8,128)(2,1)}, bf16[1024,128]{1,0:T(8,128)(2,1)S(1)}, u32[]{:S(2)}, u32[]{:S(2)}) collective-permute-start(bf16[1024,128]{1,0:T(8,128)(2,1)} %refs_0_.3), channel_id=1, source_target_pairs={{0,2},{1,3},{2,0},{3,1},{4,6},{5,7},{6,4},{7,5},{8,10},{9,11},{10,... | collective-permute-start | bytes 786440 | tf_op jit(solution)/shard_map/ppermute | solution.py:467
  6.8 53.4 %collective-permute-start.1 = (bf16[1024,128]{1,0:T(8,128)(2,1)}, bf16[1024,128]{1,0:T(8,128)(2,1)S(1)}, u32[]{:S(2)}, u32[]{:S(2)}) collective-permute-start(bf16[1024,128]{1,0:T(8,128)(2,1)} %refs_0_.3), channel_id=1, source_target_pairs={{0,4},{1,5},{2,6},{3,7},{4,0},{5,1},{6,2},{7,3},{8,12},{9,13},{10,... | collective-permute-start | bytes 786440 | tf_op jit(solution)/shard_map/ppermute | solution.py:467
  16.6 18.7 %collective-permute-start.9 = (bf16[1024,128]{1,0:T(8,128)(2,1)S(1)}, bf16[1024,128]{1,0:T(8,128)(2,1)S(1)}, u32[]{:S(2)}, u32[]{:S(2)}) collective-permute-start(bf16[1024,128]{1,0:T(8,128)(2,1)S(1)} %collective-permute-done.7.refs_1_), channel_id=1, source_target_pairs={{0,1},{1,0},{2,3},{3,2},{4,5},{5,4},{6,7},{7,6},{8,9},{9,8},{10,11... | collective-permute-start | bytes 786440 | tf_op jit(solution)/shard_map/ppermute | solution.py:467
  19.8 15.5 %collective-permute-start.4 = (bf16[1024,128]{1,0:T(8,128)(2,1)S(1)}, bf16[1024,128]{1,0:T(8,128)(2,1)S(1)}, u32[]{:S(2)}, u32[]{:S(2)}) collective-permute-start(bf16[1024,128]{1,0:T(8,128)(2,1)S(1)} %collective-permute-done.3.refs_0_), channel_id=1, source_target_pairs={{0,2},{1,3},{2,0},{3,1},{4,6},{5,7},{6,4},{7,5},{8,10},{9,11},{10,... | collective-permute-start | bytes 786440 | tf_op jit(solution)/shard_map/ppermute | solution.py:467
  32.8 27.4 %collective-permute-start.2 = (bf16[1024,128]{1,0:T(8,128)(2,1)S(1)}, bf16[1024,128]{1,0:T(8,128)(2,1)S(1)}, u32[]{:S(2)}, u32[]{:S(2)}) collective-permute-start(bf16[1024,128]{1,0:T(8,128)(2,1)S(1)} %copy-done), channel_id=1, source_target_pairs={{0,6},{1,7},{2,4},{3,5},{4,2},{5,3},{6,0},{7,1},{8,14},{9,15},{10,... | collective-permute-start | bytes 786440 | tf_op jit(solution)/shard_map/ppermute | solution.py:467
  35.3 12.4 %collective-permute-start.5 = (bf16[1024,128]{1,0:T(8,128)(2,1)S(1)}, bf16[1024,128]{1,0:T(8,128)(2,1)S(1)}, u32[]{:S(2)}, u32[]{:S(2)}) collective-permute-start(bf16[1024,128]{1,0:T(8,128)(2,1)S(1)} %collective-permute-done.3.refs_0_), channel_id=1, source_target_pairs={{0,1},{1,0},{2,3},{3,2},{4,5},{5,4},{6,7},{7,6},{8,9},{9,8},{10,11... | collective-permute-start | bytes 786440 | tf_op jit(solution)/shard_map/ppermute | solution.py:467
  35.3 12.6 %collective-permute-start.6 = (bf16[1024,128]{1,0:T(8,128)(2,1)S(1)}, bf16[1024,128]{1,0:T(8,128)(2,1)S(1)}, u32[]{:S(2)}, u32[]{:S(2)}) collective-permute-start(bf16[1024,128]{1,0:T(8,128)(2,1)S(1)} %collective-permute-done.4.refs_1_), channel_id=1, source_target_pairs={{0,1},{1,0},{2,3},{3,2},{4,5},{5,4},{6,7},{7,6},{8,9},{9,8},{10,11... | collective-permute-start | bytes 786440 | tf_op jit(solution)/shard_map/ppermute | solution.py:467
  47.7 16.0 %collective-permute-start.13 = (bf16[1024,128]{1,0:T(8,128)(2,1)S(1)}, bf16[1024,128]{1,0:T(8,128)(2,1)S(1)}, u32[]{:S(2)}, u32[]{:S(2)}) collective-permute-start(bf16[1024,128]{1,0:T(8,128)(2,1)S(1)} %copy-done), channel_id=1, source_target_pairs={{0,1},{1,0},{2,3},{3,2},{4,5},{5,4},{6,7},{7,6},{8,9},{9,8},{10,11... | collective-permute-start | bytes 786440 | tf_op jit(solution)/shard_map/ppermute | solution.py:467
  60.3 4.0 %collective-permute-start.14 = (bf16[1024,128]{1,0:T(8,128)(2,1)S(1)}, bf16[1024,128]{1,0:T(8,128)(2,1)S(1)}, u32[]{:S(2)}, u32[]{:S(2)}) collective-permute-start(bf16[1024,128]{1,0:T(8,128)(2,1)S(1)} %collective-permute-done.refs_1_), channel_id=1, source_target_pairs={{0,1},{1,0},{2,3},{3,2},{4,5},{5,4},{6,7},{7,6},{8,9},{9,8},{10,11... | collective-permute-start | bytes 786440 | tf_op jit(solution)/shard_map/ppermute | solution.py:467
  60.8 4.0 %collective-permute-start.15 = (bf16[1024,128]{1,0:T(8,128)(2,1)S(1)}, bf16[1024,128]{1,0:T(8,128)(2,1)S(1)}, u32[]{:S(2)}, u32[]{:S(2)}) collective-permute-start(bf16[1024,128]{1,0:T(8,128)(2,1)S(1)} %collective-permute-done.1.refs_2_), channel_id=1, source_target_pairs={{0,1},{1,0},{2,3},{3,2},{4,5},{5,4},{6,7},{7,6},{8,9},{9,8},{10,11... | collective-permute-start | bytes 786440 | tf_op jit(solution)/shard_map/ppermute | solution.py:467
  60.8 3.9 %collective-permute-start.16 = (bf16[1024,128]{1,0:T(8,128)(2,1)S(1)}, bf16[1024,128]{1,0:T(8,128)(2,1)S(1)}, u32[]{:S(2)}, u32[]{:S(2)}) collective-permute-start(bf16[1024,128]{1,0:T(8,128)(2,1)S(1)} %collective-permute-done.2.refs_3_), channel_id=1, source_target_pairs={{0,1},{1,0},{2,3},{3,2},{4,5},{5,4},{6,7},{7,6},{8,9},{9,8},{10,11... | collective-permute-start | bytes 786440 | tf_op jit(solution)/shard_map/ppermute | solution.py:467
  61.3 13.5 %collective-permute-start.12 = (f32[1,8192]{1,0:T(1,128)S(1)}, f32[1,8192]{1,0:T(1,128)S(1)}, u32[]{:S(2)}, u32[]{:S(2)}) collective-permute-start(f32[1,8192]{1,0:T(1,128)S(1)} %get-tuple-element.70.refs_0_), channel_id=1, source_target_pairs={{0,24},{8,16},{16,8},{24,0},{1,25},{9,17},{17,9},{25,1},{2,26},{10... | collective-permute-start | bytes 98312 | tf_op jit(solution)/shard_map/ppermute | solution.py:467
  63.7 11.1 %collective-permute-start.10 = (f32[1,8192]{1,0:T(1,128)S(1)}, f32[1,8192]{1,0:T(1,128)S(1)}, u32[]{:S(2)}, u32[]{:S(2)}) collective-permute-start(f32[1,8192]{1,0:T(1,128)S(1)} %get-tuple-element.70.refs_0_), channel_id=1, source_target_pairs={{0,8},{8,0},{16,24},{24,16},{1,9},{9,1},{17,25},{25,17},{2,10},{10... | collective-permute-start | bytes 98312 | tf_op jit(solution)/shard_map/ppermute | solution.py:467
  64.3 10.5 %collective-permute-start.11 = (f32[1,8192]{1,0:T(1,128)S(1)}, f32[1,8192]{1,0:T(1,128)S(1)}, u32[]{:S(2)}, u32[]{:S(2)}) collective-permute-start(f32[1,8192]{1,0:T(1,128)S(1)} %get-tuple-element.70.refs_0_), channel_id=1, source_target_pairs={{0,16},{8,24},{16,0},{24,8},{1,17},{9,25},{17,1},{25,9},{2,18},{10... | collective-permute-start | bytes 98312 | tf_op jit(solution)/shard_map/ppermute | solution.py:467
  77.8 1.2 collective-permute-start.17
  78.9 12.1 %collective-permute-start.20 = (f32[8,128]{1,0:T(8,128)S(1)}, f32[8,128]{1,0:T(8,128)S(1)}, u32[]{:S(2)}, u32[]{:S(2)}) collective-permute-start(f32[8,128]{1,0:T(8,128)S(1)} %add.18.refs_0_), channel_id=1, source_target_pairs={{0,6},{1,7},{2,4},{3,5},{4,2},{5,3},{6,0},{7,1},{8,14},{9,15},{10,... | collective-permute-start | bytes 12296 | tf_op jit(solution)/shard_map/ppermute | solution.py:467
  80.3 10.7 %collective-permute-start.18 = (f32[8,128]{1,0:T(8,128)S(1)}, f32[8,128]{1,0:T(8,128)S(1)}, u32[]{:S(2)}, u32[]{:S(2)}) collective-permute-start(f32[8,128]{1,0:T(8,128)S(1)} %add.18.refs_0_), channel_id=1, source_target_pairs={{0,2},{1,3},{2,0},{3,1},{4,6},{5,7},{6,4},{7,5},{8,10},{9,11},{10,... | collective-permute-start | bytes 12296 | tf_op jit(solution)/shard_map/ppermute | solution.py:467
  80.5 10.6 %collective-permute-start.19 = (f32[8,128]{1,0:T(8,128)S(1)}, f32[8,128]{1,0:T(8,128)S(1)}, u32[]{:S(2)}, u32[]{:S(2)}) collective-permute-start(f32[8,128]{1,0:T(8,128)S(1)} %add.18.refs_0_), channel_id=1, source_target_pairs={{0,4},{1,5},{2,6},{3,7},{4,0},{5,1},{6,2},{7,3},{8,12},{9,13},{10,... | collective-permute-start | bytes 12296 | tf_op jit(solution)/shard_map/ppermute | solution.py:467
  93.9 11.3 %collective-permute-start.23 = (f32[1,8192]{1,0:T(1,128)S(1)}, f32[1,8192]{1,0:T(1,128)S(1)}, u32[]{:S(2)}, u32[]{:S(2)}) collective-permute-start(f32[1,8192]{1,0:T(1,128)S(1)} %shard_map.59.refs_0_), channel_id=1, source_target_pairs={{0,24},{8,16},{16,8},{24,0},{1,25},{9,17},{17,9},{25,1},{2,26},{10... | collective-permute-start | bytes 98312 | tf_op jit(solution)/shard_map/ppermute | solution.py:467
  96.4 8.8 %collective-permute-start.21 = (f32[1,8192]{1,0:T(1,128)S(1)}, f32[1,8192]{1,0:T(1,128)S(1)}, u32[]{:S(2)}, u32[]{:S(2)}) collective-permute-start(f32[1,8192]{1,0:T(1,128)S(1)} %shard_map.59.refs_0_), channel_id=1, source_target_pairs={{0,8},{8,0},{16,24},{24,16},{1,9},{9,1},{17,25},{25,17},{2,10},{10... | collective-permute-start | bytes 98312 | tf_op jit(solution)/shard_map/ppermute | solution.py:467
  97.0 8.2 %collective-permute-start.22 = (f32[1,8192]{1,0:T(1,128)S(1)}, f32[1,8192]{1,0:T(1,128)S(1)}, u32[]{:S(2)}, u32[]{:S(2)}) collective-permute-start(f32[1,8192]{1,0:T(1,128)S(1)} %shard_map.59.refs_0_), channel_id=1, source_target_pairs={{0,16},{8,24},{16,0},{24,8},{1,17},{9,25},{17,1},{25,9},{2,18},{10... | collective-permute-start | bytes 98312 | tf_op jit(solution)/shard_map/ppermute | solution.py:467
  108.2 1.2 collective-permute-start.24
  109.4 8.2 %collective-permute-start.27 = (f32[8,128]{1,0:T(8,128)S(1)}, f32[8,128]{1,0:T(8,128)S(1)}, u32[]{:S(2)}, u32[]{:S(2)}) collective-permute-start(f32[8,128]{1,0:T(8,128)S(1)} %add.19.refs_0_), channel_id=1, source_target_pairs={{0,6},{1,7},{2,4},{3,5},{4,2},{5,3},{6,0},{7,1},{8,14},{9,15},{10,... | collective-permute-start | bytes 12296 | tf_op jit(solution)/shard_map/ppermute | solution.py:467
  110.8 6.8 %collective-permute-start.25 = (f32[8,128]{1,0:T(8,128)S(1)}, f32[8,128]{1,0:T(8,128)S(1)}, u32[]{:S(2)}, u32[]{:S(2)}) collective-permute-start(f32[8,128]{1,0:T(8,128)S(1)} %add.19.refs_0_), channel_id=1, source_target_pairs={{0,2},{1,3},{2,0},{3,1},{4,6},{5,7},{6,4},{7,5},{8,10},{9,11},{10,... | collective-permute-start | bytes 12296 | tf_op jit(solution)/shard_map/ppermute | solution.py:467
  110.8 6.8 %collective-permute-start.26 = (f32[8,128]{1,0:T(8,128)S(1)}, f32[8,128]{1,0:T(8,128)S(1)}, u32[]{:S(2)}, u32[]{:S(2)}) collective-permute-start(f32[8,128]{1,0:T(8,128)S(1)} %add.19.refs_0_), channel_id=1, source_target_pairs={{0,4},{1,5},{2,6},{3,7},{4,0},{5,1},{6,2},{7,3},{8,12},{9,13},{10,... | collective-permute-start | bytes 12296 | tf_op jit(solution)/shard_map/ppermute | solution.py:467
  120.4 7.3 %collective-permute-start.30 = (f32[1,8192]{1,0:T(1,128)S(1)}, f32[1,8192]{1,0:T(1,128)S(1)}, u32[]{:S(2)}, u32[]{:S(2)}) collective-permute-start(f32[1,8192]{1,0:T(1,128)S(1)} %shard_map.64.refs_0_), channel_id=1, source_target_pairs={{0,24},{8,16},{16,8},{24,0},{1,25},{9,17},{17,9},{25,1},{2,26},{10... | collective-permute-start | bytes 98312 | tf_op jit(solution)/shard_map/ppermute | solution.py:467
  122.9 4.8 %collective-permute-start.28 = (f32[1,8192]{1,0:T(1,128)S(1)}, f32[1,8192]{1,0:T(1,128)S(1)}, u32[]{:S(2)}, u32[]{:S(2)}) collective-permute-start(f32[1,8192]{1,0:T(1,128)S(1)} %shard_map.64.refs_0_), channel_id=1, source_target_pairs={{0,8},{8,0},{16,24},{24,16},{1,9},{9,1},{17,25},{25,17},{2,10},{10... | collective-permute-start | bytes 98312 | tf_op jit(solution)/shard_map/ppermute | solution.py:467
  123.5 4.3 %collective-permute-start.29 = (f32[1,8192]{1,0:T(1,128)S(1)}, f32[1,8192]{1,0:T(1,128)S(1)}, u32[]{:S(2)}, u32[]{:S(2)}) collective-permute-start(f32[1,8192]{1,0:T(1,128)S(1)} %shard_map.64.refs_0_), channel_id=1, source_target_pairs={{0,16},{8,24},{16,0},{24,8},{1,17},{9,25},{17,1},{25,9},{2,18},{10... | collective-permute-start | bytes 98312 | tf_op jit(solution)/shard_map/ppermute | solution.py:467
  137.2 1.2 collective-permute-start.31
  138.5 4.4 %collective-permute-start.32 = (f32[24,128]{1,0:T(8,128)S(1)}, f32[24,128]{1,0:T(8,128)S(1)}, u32[]{:S(2)}, u32[]{:S(2)}) collective-permute-start(f32[24,128]{1,0:T(8,128)S(1)} %add.20.refs_0_), channel_id=1, source_target_pairs={{0,2},{1,3},{2,0},{3,1},{4,6},{5,7},{6,4},{7,5},{8,10},{9,11},{10,... | collective-permute-start | bytes 36872 | tf_op jit(solution)/shard_map/ppermute | solution.py:467
  138.5 4.6 %collective-permute-start.33 = (f32[24,128]{1,0:T(8,128)S(1)}, f32[24,128]{1,0:T(8,128)S(1)}, u32[]{:S(2)}, u32[]{:S(2)}) collective-permute-start(f32[24,128]{1,0:T(8,128)S(1)} %add.20.refs_0_), channel_id=1, source_target_pairs={{0,4},{1,5},{2,6},{3,7},{4,0},{5,1},{6,2},{7,3},{8,12},{9,13},{10,... | collective-permute-start | bytes 36872 | tf_op jit(solution)/shard_map/ppermute | solution.py:467
  140.5 5.5 %collective-permute-start.34 = (f32[24,128]{1,0:T(8,128)S(1)}, f32[24,128]{1,0:T(8,128)S(1)}, u32[]{:S(2)}, u32[]{:S(2)}) collective-permute-start(f32[24,128]{1,0:T(8,128)S(1)} %add.20.refs_0_), channel_id=1, source_target_pairs={{0,6},{1,7},{2,4},{3,5},{4,2},{5,3},{6,0},{7,1},{8,14},{9,15},{10,... | collective-permute-start | bytes 36872 | tf_op jit(solution)/shard_map/ppermute | solution.py:467

commit v2 on v1

--- a/solution.py
+++ b/solution.py
@@ -66,7 +66,25 @@
     return pltpu.make_async_copy(src.at[rows, :], buf.at[slot], sems.at[slot])
 
 
-def norm_kernel(tile, depth, p_ref, u_ref, buf, obuf, inv, sems, osems):
+def position(fast):
+    if not fast:
+        return 0, 0
+    me = lax.axis_index("proto")
+    return lax.div(me, 2), lax.rem(me, 2)
+
+
+def unit_copies(fast, slots, start, unit, buf, sems):
+    z = position(fast)[0]
+    count = buf.shape[1]
+    return [
+        pltpu.make_async_copy(
+            unit.at[lax.bitwise_xor(z, s) if fast else s, pl.ds(start, count), :], buf.at[n], sems.at[n]
+        )
+        for n, s in enumerate(slots)
+    ]
+
+
+def norm_kernel(fast, slots, tile, depth, p_ref, u_ref, ahead, buf, obuf, inv, sems, osems, asems):
     total = p_ref.shape[0]
     steps = total // tile
     width = p_ref.shape[1] // CHUNKS
@@ -115,8 +133,17 @@
         return carry
 
     lax.fori_loop(0, steps, step, 0)
+    copies = unit_copies(fast, slots, 0, u_ref, ahead, asems)
+    early = steps - depth >= -(-ahead.shape[1] // tile)
+    if early:
+        for c in copies:
+            c.start()
     for i in range(max(steps - depth, 0), steps):
         store(i, i % depth).wait()
+    for c in copies:
+        if not early:
+            c.start()
+        c.wait()
 
 
 def order(fast, core, own, sib):
@@ -125,46 +152,32 @@
     return jnp.where(core == 0, own, sib), jnp.where(core == 0, sib, own)
 
 
-def position(fast):
-    if not fast:
-        return 0, 0
-    me = lax.axis_index("proto")
-    return lax.div(me, 2), lax.rem(me, 2)
-
-
 def square(x):
     y = x.astype(F32)
     return y * y
 
 
-def stage_kernel(fast, slots, last, scale, tile, block, *refs):
+def stage_kernel(fast, slots, follow, last, scale, tile, block, *refs):
     count = len(slots)
     own = refs[:count]
     sib = refs[count : 2 * count]
-    unit = refs[2 * count]
-    at = 2 * count + 1
+    unit, head = refs[2 * count : 2 * count + 2]
+    at = 2 * count + 2
     if last:
         sq_in = refs[at + HALVES]
         at += HALVES + 1
     k = refs[at : at + HALVES]
-    extra, lhs, inv, buf, sems, csum = refs[at + HALVES :]
-    z, core = position(fast)
+    extra, ahead, lhs, inv, buf, sems, asems, csum = refs[at + HALVES :]
+    _, core = position(fast)
     half = k[0].shape[1]
     rows_all = k[0].shape[0]
 
     def copies(h):
-        return [
-            pltpu.make_async_copy(
-                unit.at[lax.bitwise_xor(z, s) if fast else s, pl.ds(h * half, half), :],
-                buf.at[h % 2, n],
-                sems.at[h % 2, n],
-            )
-            for n, s in enumerate(slots)
-        ]
-
-    for h in range(2):
-        for c in copies(h):
-            c.start()
+        return unit_copies(fast, slots, h * half, unit, buf.at[h % 2], sems.at[h % 2])
+
+    coming = unit_copies(fast, follow, 0, unit, ahead, asems)
+    for c in copies(1):
+        c.start()
     for n in range(count):
         a, b = own[n][...], sib[n][...]
         first, second = order(fast, core, a, b)
@@ -190,17 +203,22 @@
     if last:
         csum[...] = jnp.zeros(csum.shape, F32)
     for h in range(HALVES):
-        for c in copies(h):
-            c.wait()
-
-        def body(t, carry, h=h):
+        if h:
+            for c in copies(h):
+                c.wait()
+        if h + 1 == HALVES:
+            for c in coming:
+                c.start()
+        weights = buf.at[h % 2] if h else head
+
+        def body(t, carry, h=h, weights=weights):
             rows = pl.ds(pl.multiple_of(t * block, block), block)
             for n in range(half // tile):
                 d = None
                 for i in range(count):
                     p = lax.dot_general(
                         lhs[i, rows, :],
-                        buf[h % 2, i, n * tile : (n + 1) * tile, :],
+                        weights[i, n * tile : (n + 1) * tile, :],
                         (((1,), (1,)), ((), ())),
                         preferred_element_type=F32,
                     )
@@ -219,6 +237,8 @@
         if h + 2 < HALVES:
             for c in copies(h + 2):
                 c.start()
+    for c in coming:
+        c.wait()
     if last:
         extra[...] = jnp.sum(csum[...], axis=0, keepdims=True)
 
@@ -340,24 +360,11 @@
     out[2 * blocks :, :] = rows_to_lanes(cross[...]) * (1.0 / (LOGIT_STEPS * LOG2E))
 
 
-def piece_copies(fast, z, offset, unit, buf, sems):
-    piece = buf.shape[1]
-    return [
-        pltpu.make_async_copy(
-            unit.at[lax.bitwise_xor(z, s) if fast else s, pl.ds(offset, piece), :], buf.at[s], sems.at[s]
-        )
-        for s in range(CHUNKS)
-    ]
-
-
 def prep_kernel(fast, scale, *refs):
     own = refs[:CHUNKS]
     sib = refs[CHUNKS : 2 * CHUNKS]
-    unit, lhs, inv, ahead, sems = refs[2 * CHUNKS :]
-    z, core = position(fast)
-    copies = piece_copies(fast, z, 0, unit, ahead, sems)
-    for c in copies:
-        c.start()
+    lhs, inv = refs[2 * CHUNKS :]
+    _, core = position(fast)
     width = own[0].shape[1]
     sq = jnp.zeros(inv.shape, F32)
     for s in range(CHUNKS):
@@ -368,8 +375,6 @@
         sq = sq + square(a) + square(b)
     total = jnp.sum(sq, axis=1, keepdims=True)
     inv[...] = jnp.broadcast_to(lax.rsqrt(total + NORM_EPS) * scale, inv.shape)
-    for c in copies:
-        c.wait()
 
 
 def logit_kernel(fast, offset, tile, block, *refs):
@@ -379,7 +384,7 @@
         copies = []
     else:
         unit, tot_in, tot_out, q_ref, ahead, qbuf, qsems, sems = refs[3:]
-        copies = piece_copies(fast, position(fast)[0], offset, unit, ahead, sems)
+        copies = unit_copies(fast, range(CHUNKS), offset, unit, ahead, sems)
     rows_all, piece = q_ref.shape
     steps = piece // tile
 
@@ -447,13 +452,14 @@
         def _():
             copy(i - depth, slot).wait()
 
-        rows = pl.ds(pl.multiple_of(i * tile, tile), tile)
-        r = rb[rows, :]
-        for h in range(HALVES):
-            for n in range(half // LANES):
-                oc = slice(h * half + n * LANES, h * half + (n + 1) * LANES)
-                x = k[h][rows, n * LANES : (n + 1) * LANES]
-                buf[slot, :, oc] = (x * c_ref[:, oc] * r).astype(BF16)
+        for u in range(tile // 16):
+            rows = pl.ds(pl.multiple_of(i * tile + u * 16, 16), 16)
+            r = rb[rows, :]
+            for h in range(HALVES):
+                for n in range(half // LANES):
+                    oc = slice(h * half + n * LANES, h * half + (n + 1) * LANES)
+                    x = k[h][rows, n * LANES : (n + 1) * LANES]
+                    buf[slot, u * 16 : u * 16 + 16, oc] = (x * c_ref[:, oc] * r).astype(BF16)
         copy(i, slot).start()
         return carry
 
@@ -523,9 +529,13 @@
     packed = sds((rows // LANES, LANES), F32)
 
     ntile = min(512, half)
-    unit = call(
-        functools.partial(norm_kernel, ntile, 4),
-        pltpu.HBM((CHUNKS, cols, width), BF16),
+    per_stage = CHUNKS // 2
+    slots = [tuple(range(s * per_stage, (s + 1) * per_stage)) for s in range(2)] + [tuple(range(CHUNKS))]
+    stage_shape = sds((per_stage, half, width), BF16)
+    ahead_shape = sds((CHUNKS, piece, width), BF16)
+    unit, ahead = call(
+        functools.partial(norm_kernel, fast, slots[0], ntile, 4),
+        (pltpu.HBM((CHUNKS, cols, width), BF16), stage_shape),
         [HB],
         (prototypes,),
         scratch=[
@@ -534,6 +544,7 @@
             pltpu.VMEM((ntile, LANES), F32),
             pltpu.SemaphoreType.DMA((4,)),
             pltpu.SemaphoreType.DMA((4,)),
+            pltpu.SemaphoreType.DMA((per_stage,)),
         ],
         limit=14,
         flops=5e9,
@@ -547,21 +558,20 @@
     tile = min(256, piece)
     kshape = tuple(pltpu.VMEM((rows, half), F32) for _ in range(HALVES))
     k, extra = (), ()
-    per_stage = CHUNKS // 2
     for s in range(2):
         last = s == 1
-        slots = tuple(range(s * per_stage, (s + 1) * per_stage))
-        nin = 2 * per_stage + 1
-        res = call(
-            functools.partial(stage_kernel, fast, slots, last, LOG2E / EPSILON, tile, block),
-            kshape + (vec if last else sds((rows, LANES), F32),),
-            [VM] * (nin - 1) + [HB] + [VM] * (HALVES + 1 if last else 0),
-            (*[own1[i] for i in slots], *[sib1[i] for i in slots], unit, *k, *extra),
+        nin = 2 * per_stage + 2
+        *res, ahead = call(
+            functools.partial(stage_kernel, fast, slots[s], slots[s + 1], last, LOG2E / EPSILON, tile, block),
+            kshape + (vec if last else sds((rows, LANES), F32), ahead_shape if last else stage_shape),
+            [VM] * (nin - 2) + [HB, VM] + [VM] * (HALVES + 1 if last else 0),
+            (*[own1[i] for i in slots[s]], *[sib1[i] for i in slots[s]], unit, ahead, *k, *extra),
             scratch=[
                 pltpu.VMEM((per_stage, rows, width), BF16),
                 pltpu.VMEM((rows, LANES), F32),
                 pltpu.VMEM((2, per_stage, half, width), BF16),
                 pltpu.SemaphoreType.DMA((2, per_stage)),
+                pltpu.SemaphoreType.DMA((CHUNKS if last else per_stage,)),
                 pltpu.VMEM((8, cols), F32),
             ],
             limit=8,
@@ -575,13 +585,11 @@
     else:
         own2, sib2 = slices_plain(predictor_view_embeddings, width // 2)
 
-    ahead_shape = sds((CHUNKS, piece, width), BF16)
-    lhs2, inv2, ahead = call(
+    lhs2, inv2 = call(
         functools.partial(prep_kernel, fast, LOG2E / SOFTMAX_TEMP_VALUE),
-        (sds((CHUNKS, rows, width), BF16), sds((rows, LANES), F32), ahead_shape),
-        [VM] * (2 * CHUNKS) + [HB],
-        (*own2, *sib2, unit),
-        scratch=[pltpu.SemaphoreType.DMA((CHUNKS,))],
+        (sds((CHUNKS, rows, width), BF16), sds((rows, LANES), F32)),
+        [VM] * (2 * CHUNKS),
+        (*own2, *sib2),
         flops=5e8,
     )
     tot = jnp.zeros((rows, LANES), F32)

time: 154 us -> 152 us (0.987)
  Pallas kernels: 98.6 us -> 96.2 us
    pallas_call x18, Pallas kernels: 98.6 us -> 96.2 us  [call(): pl.pallas_call(kernel, out_shape=outs, in_specs=ins, out_specs=jax.tree.m...]
where the time goes in v2:
time: 152 us
  Pallas kernels  96.2 us (63%)
  starting transfers between devices  34.2 us (23%)
  waiting for transfers between devices  19.6 us (13%)
    pallas_call x18, Pallas kernels, call(): pl.pallas_call(kernel, out_shape=outs, in_specs=ins, out_specs=jax.tree.m...  96.2 us
    ppermute x35, starting transfers between devices, swap(): return lax.ppermute(x, axis, [(i, i ^ distance) for i in range(n)])  34.2 us
    ppermute x35, waiting for transfers between devices, swap(): return lax.ppermute(x, axis, [(i, i ^ distance) for i in range(n)])  19.6 us
  transfers between devices with their start and end apart: 35, of which 7 were waited for; matrix products, arithmetic and copies ran while one was open for 0% of the time, Pallas kernels for 45%

profile of v2, /device:TPU:0, one launch (start us, length us, event | category | flops | bytes accessed | tf_op | source)
XLA Modules:
  0.0 151.8 jit_solution(17880683561816611163)
XLA Ops:
  0.6 3.1 %collective-permute-start.7 = (bf16[1024,128]{1,0:T(8,128)(2,1)}, bf16[1024,128]{1,0:T(8,128)(2,1)S(1)}, u32[]{:S(2)}, u32[]{:S(2)}) collective-permute-start(bf16[1024,128]{1,0:T(8,128)(2,1)} %refs_0_.2), channel_id=1, source_target_pairs={{0,2},{1,3},{2,0},{3,1},{4,6},{5,7},{6,4},{7,5},{8,10},{9,11},{10,... | collective-permute-start | bytes 786440 | tf_op jit(solution)/shard_map/ppermute | solution.py:473
  3.8 2.6 %collective-permute-start.3 = (bf16[1024,128]{1,0:T(8,128)(2,1)}, bf16[1024,128]{1,0:T(8,128)(2,1)S(1)}, u32[]{:S(2)}, u32[]{:S(2)}) collective-permute-start(bf16[1024,128]{1,0:T(8,128)(2,1)} %refs_0_.2), channel_id=1, source_target_pairs={{0,4},{1,5},{2,6},{3,7},{4,0},{5,1},{6,2},{7,3},{8,12},{9,13},{10,... | collective-permute-start | bytes 786440 | tf_op jit(solution)/shard_map/ppermute | solution.py:473
  6.4 0.0 collective-permute-start.8
  6.4 0.4 collective-permute-start
  6.8 0.0 collective-permute-start.1
  6.8 9.8 %collective-permute-done.7.refs_1_ = bf16[1024,128]{1,0:T(8,128)(2,1)S(1)} collective-permute-done((bf16[1024,128]{1,0:T(8,128)(2,1)}, bf16[1024,128]{1,0:T(8,128)(2,1)S(1)}, u32[]{:S(2)}, u32[]{:S(2)}) %collective-permute-start.7) | collective-permute-done | bytes 262176 | tf_op jit(solution)/shard_map/ppermute | solution.py:473
  16.6 3.2 %collective-permute-done.3.refs_0_ = bf16[1024,128]{1,0:T(8,128)(2,1)S(1)} collective-permute-done((bf16[1024,128]{1,0:T(8,128)(2,1)}, bf16[1024,128]{1,0:T(8,128)(2,1)S(1)}, u32[]{:S(2)}, u32[]{:S(2)}) %collective-permute-start.3) | collective-permute-done | bytes 262176 | tf_op jit(solution)/shard_map/ppermute | solution.py:473
  19.8 0.1 collective-permute-start.4
  19.8 13.9 %shard_map.50 = (bf16[4,8192,256]{2,1,0:T(8,128)(2,1)}, bf16[2,2048,256]{2,1,0:T(8,128)(2,1)S(1)}) custom-call(bf16[8192,1024]{1,0:T(8,128)(2,1)} %p_ref.1), custom_call_target="tpu_custom_call" | custom-call | flops 5000000000 | tf_op jit(solution)/shard_map/pallas_call | solution.py:36
  33.8 2.5 %collective-permute-start.2 = (bf16[1024,128]{1,0:T(8,128)(2,1)S(1)}, bf16[1024,128]{1,0:T(8,128)(2,1)S(1)}, u32[]{:S(2)}, u32[]{:S(2)}) collective-permute-start(bf16[1024,128]{1,0:T(8,128)(2,1)S(1)} %copy-done), channel_id=1, source_target_pairs={{0,6},{1,7},{2,4},{3,5},{4,2},{5,3},{6,0},{7,1},{8,14},{9,15},{10,... | collective-permute-start | bytes 786440 | tf_op jit(solution)/shard_map/ppermute | solution.py:473
  36.2 0.0 collective-permute-start.5
  36.3 0.0 collective-permute-done.4.refs_1_
  36.3 0.5 collective-permute-start.6
  36.8 10.8 %shard_map.51 = (f32[1024,2048]{1,0:T(8,128)S(1)}, f32[1024,2048]{1,0:T(8,128)S(1)}, f32[1024,2048]{1,0:T(8,128)S(1)}, f32[1024,2048]{1,0:T(8,128)S(1)}, f32[102...) custom-call(bf16[1024,128]{1,0:T(8,128)(2,1)S(1)} %copy-done.1, ...), custom_call_target="tpu_custom_call" | custom-call | flops 8589934592 | tf_op jit(solution)/shard_map/pallas_call | solution.py:36
  47.6 0.1 collective-permute-start.13
  47.7 11.7 %shard_map.52 = (f32[1024,2048]{1,0:T(8,128)S(1)}, f32[1024,2048]{1,0:T(8,128)S(1)}, f32[1024,2048]{1,0:T(8,128)S(1)}, f32[1024,2048]{1,0:T(8,128)S(1)}, f32[1,8...) custom-call(bf16[1024,128]{1,0:T(8,128)(2,1)S(1)} %collective-permut, ...), custom_call_target="tpu_custom_call", output_to_operand_aliasing={{0}: (6, {}), {1}: (7, {}), {2}: (8, {}), {3}: (9, {})} | custom-call | flops 8589934592 | tf_op jit(solution)/shard_map/pallas_call | solution.py:36
  59.4 0.0 collective-permute-done.1.refs_2_
  59.4 0.0 collective-permute-done.2.refs_3_
  59.4 0.5 collective-permute-start.14
  59.9 0.1 collective-permute-start.15
  60.0 0.4 collective-permute-start.16
  60.4 2.4 %collective-permute-start.12 = (f32[1,8192]{1,0:T(1,128)S(1)}, f32[1,8192]{1,0:T(1,128)S(1)}, u32[]{:S(2)}, u32[]{:S(2)}) collective-permute-start(f32[1,8192]{1,0:T(1,128)S(1)} %get-tuple-element.76.refs_0_), channel_id=1, source_target_pairs={{0,24},{8,16},{16,8},{24,0},{1,25},{9,17},{17,9},{25,1},{2,26},{10... | collective-permute-start | bytes 98312 | tf_op jit(solution)/shard_map/ppermute | solution.py:473
  62.9 0.5 collective-permute-start.10
  63.4 0.5 collective-permute-start.11
  64.0 0.6 shard_map.53
  64.6 3.8 %shard_map.54 = (f32[1024,128]{1,0:T(8,128)S(1)}, s16[1024,1024]{1,0:T(8,128)(2,1)}, bf16[4,1024,256]{2,1,0:T(8,128)(2,1)S(1)}) custom-call(bf16[4,1024,256]{2,1,0:T(8,128)(2,1)S(1)} %get-tuple-element.80.refs_0_, f32[1024,128]{1,0:T(8,128)S(1)} %get-tuple-element.81.refs_1_, bf16[4,1024,256]{2,1,0:T(8,128)(2,1)S(1)} %get-tuple-element.82.refs_2_, ...), custom_call_target="tpu_custom_call" | custom-call | flops 2147483648 | tf_op jit(solution)/shard_map/pallas_call | solution.py:36
  68.5 4.0 %shard_map.55 = (f32[1024,128]{1,0:T(8,128)S(1)}, s16[1024,1024]{1,0:T(8,128)(2,1)}, bf16[4,1024,256]{2,1,0:T(8,128)(2,1)S(1)}) custom-call(bf16[4,1024,256]{2,1,0:T(8,128)(2,1)S(1)} %get-tuple-element.80.refs_0_, f32[1024,128]{1,0:T(8,128)S(1)} %get-tuple-element.81.refs_1_, bf16[4,1024,256]{2,1,0:T(8,128)(2,1)S(1)} %get-tuple-element.84.refs_2_, ...), custom_call_target="tpu_custom_call" | custom-call | flops 2147483648 | tf_op jit(solution)/shard_map/pallas_call | solution.py:36
  72.5 0.0 collective-permute-done.12.refs_3_
  72.5 0.0 collective-permute-done.10.refs_1_
  72.5 3.0 %shard_map.56 = (f32[8,128]{1,0:T(8,128)S(1)}, f32[1,8192]{1,0:T(1,128)}) custom-call(f32[1,8192]{1,0:T(1,128)S(1)} %get-tuple-element.76.refs_0_, f32[1,8192]{1,0:T(1,128)S(1)} %collective-permute-done.10.refs_1_, f32[1,8192]{1,0:T(1,128)S(1)} %collective-permute-done.11.refs_2_, f32[1,8192]{1,0:T(1,128)S(1)} %collective-permute-done.12.refs_3_, ...), custom_call_target="tpu_custom_call" | custom-call | flops 4000000000 | tf_op jit(solution)/shard_map/pallas_call | solution.py:36
  75.5 1.2 collective-permute-done.17
  76.6 1.4 collective-permute-start.20
  78.1 0.2 collective-permute-start.18
  78.2 2.8 %collective-permute-start.19 = (f32[8,128]{1,0:T(8,128)S(1)}, f32[8,128]{1,0:T(8,128)S(1)}, u32[]{:S(2)}, u32[]{:S(2)}) collective-permute-start(f32[8,128]{1,0:T(8,128)S(1)} %add.18.refs_0_), channel_id=1, source_target_pairs={{0,4},{1,5},{2,6},{3,7},{4,0},{5,1},{6,2},{7,3},{8,12},{9,13},{10,... | collective-permute-start | bytes 12296 | tf_op jit(solution)/shard_map/ppermute | solution.py:473
  81.0 3.8 %shard_map.57 = (f32[1024,128]{1,0:T(8,128)S(1)}, s16[1024,1024]{1,0:T(8,128)(2,1)}, bf16[4,1024,256]{2,1,0:T(8,128)(2,1)S(1)}) custom-call(bf16[4,1024,256]{2,1,0:T(8,128)(2,1)S(1)} %get-tuple-element.80.refs_0_, f32[1024,128]{1,0:T(8,128)S(1)} %get-tuple-element.81.refs_1_, bf16[4,1024,256]{2,1,0:T(8,128)(2,1)S(1)} %get-tuple-element.94.refs_2_, ...), custom_call_target="tpu_custom_call" | custom-call | flops 2147483648 | tf_op jit(solution)/shard_map/pallas_call | solution.py:36
  84.9 3.9 %shard_map.58 = (f32[1024,128]{1,0:T(8,128)S(1)}, s16[1024,1024]{1,0:T(8,128)(2,1)}, bf16[4,1024,256]{2,1,0:T(8,128)(2,1)S(1)}) custom-call(bf16[4,1024,256]{2,1,0:T(8,128)(2,1)S(1)} %get-tuple-element.80.refs_0_, f32[1024,128]{1,0:T(8,128)S(1)} %get-tuple-element.81.refs_1_, bf16[4,1024,256]{2,1,0:T(8,128)(2,1)S(1)} %get-tuple-element.97.refs_2_, ...), custom_call_target="tpu_custom_call" | custom-call | flops 2147483648 | tf_op jit(solution)/shard_map/pallas_call | solution.py:36
  88.7 0.0 collective-permute-done.20.refs_3_
  88.8 0.0 collective-permute-done.19.refs_2_
  88.8 2.8 %shard_map.59.refs_0_ = f32[1,8192]{1,0:T(1,128)S(1)} custom-call(f32[8,128]{1,0:T(8,128)S(1)} %add.18.refs_0_, f32[8,128]{1,0:T(8,128)S(1)} %collective-permute-done.18.refs_1_, f32[8,128]{1,0:T(8,128)S(1)} %collective-permute-done.19.refs_2_, f32[8,128]{1,0:T(8,128)S(1)} %collective-permute-done.20.refs_3_, f32[1024,2048]{1,0:T(8,128)S(1)} %get-tuple-element.89.refs_4_, ...), custom_call_target="tpu_custom_call" | custom-call | flops 4000000000 | tf_op jit(solution)/shard_map/pallas_call | solution.py:36
  91.6 2.5 %collective-permute-start.23 = (f32[1,8192]{1,0:T(1,128)S(1)}, f32[1,8192]{1,0:T(1,128)S(1)}, u32[]{:S(2)}, u32[]{:S(2)}) collective-permute-start(f32[1,8192]{1,0:T(1,128)S(1)} %shard_map.59.refs_0_), channel_id=1, source_target_pairs={{0,24},{8,16},{16,8},{24,0},{1,25},{9,17},{17,9},{25,1},{2,26},{10... | collective-permute-start | bytes 98312 | tf_op jit(solution)/shard_map/ppermute | solution.py:473
  94.1 0.5 collective-permute-start.21
  94.7 0.5 collective-permute-start.22
  95.2 3.8 %shard_map.60 = (f32[1024,128]{1,0:T(8,128)S(1)}, s16[1024,1024]{1,0:T(8,128)(2,1)}, bf16[4,1024,256]{2,1,0:T(8,128)(2,1)S(1)}) custom-call(bf16[4,1024,256]{2,1,0:T(8,128)(2,1)S(1)} %get-tuple-element.80.refs_0_, f32[1024,128]{1,0:T(8,128)S(1)} %get-tuple-element.81.refs_1_, bf16[4,1024,256]{2,1,0:T(8,128)(2,1)S(1)} %get-tuple-element.102.refs_2_, ...), custom_call_target="tpu_custom_call" | custom-call | flops 2147483648 | tf_op jit(solution)/shard_map/pallas_call | solution.py:36
  99.0 3.9 %shard_map.61 = (f32[1024,128]{1,0:T(8,128)S(1)}, s16[1024,1024]{1,0:T(8,128)(2,1)}, bf16[4,1024,256]{2,1,0:T(8,128)(2,1)S(1)}) custom-call(bf16[4,1024,256]{2,1,0:T(8,128)(2,1)S(1)} %get-tuple-element.80.refs_0_, f32[1024,128]{1,0:T(8,128)S(1)} %get-tuple-element.81.refs_1_, bf16[4,1024,256]{2,1,0:T(8,128)(2,1)S(1)} %get-tuple-element.105.refs_2_, ...), custom_call_target="tpu_custom_call" | custom-call | flops 2147483648 | tf_op jit(solution)/shard_map/pallas_call | solution.py:36
  102.9 0.0 collective-permute-done.23.refs_3_
  102.9 3.0 %shard_map.62 = (f32[8,128]{1,0:T(8,128)S(1)}, f32[1,8192]{1,0:T(1,128)}) custom-call(f32[1,8192]{1,0:T(1,128)S(1)} %shard_map.59.refs_0_, f32[1,8192]{1,0:T(1,128)S(1)} %collective-permute-done.21.refs_1_, f32[1,8192]{1,0:T(1,128)S(1)} %collective-permute-done.22.refs_2_, f32[1,8192]{1,0:T(1,128)S(1)} %collective-permute-done.23.refs_3_, ...), custom_call_target="tpu_custom_call" | custom-call | flops 4000000000 | tf_op jit(solution)/shard_map/pallas_call | solution.py:36
  105.9 1.2 collective-permute-done.24
  107.0 1.4 collective-permute-start.27
  108.4 3.0 %collective-permute-start.26 = (f32[8,128]{1,0:T(8,128)S(1)}, f32[8,128]{1,0:T(8,128)S(1)}, u32[]{:S(2)}, u32[]{:S(2)}) collective-permute-start(f32[8,128]{1,0:T(8,128)S(1)} %add.19.refs_0_), channel_id=1, source_target_pairs={{0,4},{1,5},{2,6},{3,7},{4,0},{5,1},{6,2},{7,3},{8,12},{9,13},{10,... | collective-permute-start | bytes 12296 | tf_op jit(solution)/shard_map/ppermute | solution.py:473
  111.4 3.8 %shard_map.63 = (f32[1024,128]{1,0:T(8,128)S(1)}, s16[1024,1024]{1,0:T(8,128)(2,1)}, bf16[4,1024,256]{2,1,0:T(8,128)(2,1)S(1)}) custom-call(bf16[4,1024,256]{2,1,0:T(8,128)(2,1)S(1)} %get-tuple-element.80.refs_0_, f32[1024,128]{1,0:T(8,128)S(1)} %get-tuple-element.81.refs_1_, bf16[4,1024,256]{2,1,0:T(8,128)(2,1)S(1)} %get-tuple-element.111.refs_2_, ...), custom_call_target="tpu_custom_call" | custom-call | flops 2147483648 | tf_op jit(solution)/shard_map/pallas_call | solution.py:36
  115.2 2.8 %shard_map.64.refs_0_ = f32[1,8192]{1,0:T(1,128)S(1)} custom-call(f32[8,128]{1,0:T(8,128)S(1)} %add.19.refs_0_, f32[8,128]{1,0:T(8,128)S(1)} %collective-permute-done.25.refs_1_, f32[8,128]{1,0:T(8,128)S(1)} %collective-permute-done.26.refs_2_, f32[8,128]{1,0:T(8,128)S(1)} %collective-permute-done.27.refs_3_, f32[1024,2048]{1,0:T(8,128)S(1)} %get-tuple-element.89.refs_4_, ...), custom_call_target="tpu_custom_call" | custom-call | flops 4000000000 | tf_op jit(solution)/shard_map/pallas_call | solution.py:36
  118.1 2.5 %collective-permute-start.30 = (f32[1,8192]{1,0:T(1,128)S(1)}, f32[1,8192]{1,0:T(1,128)S(1)}, u32[]{:S(2)}, u32[]{:S(2)}) collective-permute-start(f32[1,8192]{1,0:T(1,128)S(1)} %shard_map.64.refs_0_), channel_id=1, source_target_pairs={{0,24},{8,16},{16,8},{24,0},{1,25},{9,17},{17,9},{25,1},{2,26},{10... | collective-permute-start | bytes 98312 | tf_op jit(solution)/shard_map/ppermute | solution.py:473
  120.6 0.5 collective-permute-start.28
  121.1 0.5 collective-permute-start.29
  121.6 3.8 %shard_map.65 = (f32[1024,128]{1,0:T(8,128)S(1)}, s16[1024,1024]{1,0:T(8,128)(2,1)}) custom-call(bf16[4,1024,256]{2,1,0:T(8,128)(2,1)S(1)} %get-tuple-element.80.refs_0_, f32[1024,128]{1,0:T(8,128)S(1)} %get-tuple-element.81.refs_1_, bf16[4,1024,256]{2,1,0:T(8,128)(2,1)S(1)} %get-tuple-element.116.refs_2_, f32[1024,128]{1,0:T(8,128)S(1)} %get-tuple-element.118.refs_3_), custom_call_target="tpu_custom_call" | custom-call | flops 2147483648 | tf_op jit(solution)/shard_map/pallas_call | solution.py:36
  125.4 9.5 %shard_map.66 = (f32[24,128]{1,0:T(8,128)S(1)}, f32[1,8192]{1,0:T(1,128)S(1)}) custom-call(f32[1,8192]{1,0:T(1,128)S(1)} %shard_map.64.refs_0_, f32[1,8192]{1,0:T(1,128)S(1)} %collective-permute-done.28.refs_1_, f32[1,8192]{1,0:T(1,128)S(1)} %collective-permute-done.29.refs_2_, f32[1,8192]{1,0:T(1,128)S(1)} %collective-permute-done.30.refs_3_, ...), custom_call_target="tpu_custom_call" | custom-call | flops 8000000000 | tf_op jit(solution)/shard_map/pallas_call | solution.py:36
  134.9 0.1 collective-permute-start.31
  135.0 1.2 collective-permute-done.31
  136.1 2.0 %collective-permute-start.33 = (f32[24,128]{1,0:T(8,128)S(1)}, f32[24,128]{1,0:T(8,128)S(1)}, u32[]{:S(2)}, u32[]{:S(2)}) collective-permute-start(f32[24,128]{1,0:T(8,128)S(1)} %add.20.refs_0_), channel_id=1, source_target_pairs={{0,4},{1,5},{2,6},{3,7},{4,0},{5,1},{6,2},{7,3},{8,12},{9,13},{10,... | collective-permute-start | bytes 36872 | tf_op jit(solution)/shard_map/ppermute | solution.py:473
  138.1 2.4 %collective-permute-start.34 = (f32[24,128]{1,0:T(8,128)S(1)}, f32[24,128]{1,0:T(8,128)S(1)}, u32[]{:S(2)}, u32[]{:S(2)}) collective-permute-start(f32[24,128]{1,0:T(8,128)S(1)} %add.20.refs_0_), channel_id=1, source_target_pairs={{0,6},{1,7},{2,4},{3,5},{4,2},{5,3},{6,0},{7,1},{8,14},{9,15},{10,... | collective-permute-start | bytes 36872 | tf_op jit(solution)/shard_map/ppermute | solution.py:473
  140.5 0.2 collective-permute-done.33.refs_2_
  140.8 2.8 %collective-permute-done.34.refs_3_ = f32[24,128]{1,0:T(8,128)S(1)} collective-permute-done((f32[24,128]{1,0:T(8,128)S(1)}, f32[24,128]{1,0:T(8,128)S(1)}, u32[]{:S(2)}, u32[]{:S(2)}) %collective-permute-start.34) | collective-permute-done | bytes 12320 | tf_op jit(solution)/shard_map/ppermute | solution.py:473
  143.6 0.6 fusion.1
  144.2 7.4 %shard_map.67 = bf16[1024,8192]{1,0:T(8,128)(2,1)} custom-call(f32[24,128]{1,0:T(8,128)S(1)} %add.20.refs_0_, f32[24,128]{1,0:T(8,128)S(1)} %collective-permute-done.32.refs_1_, f32[24,128]{1,0:T(8,128)S(1)} %collective-permute-done.33.refs_2_, f32[24,128]{1,0:T(8,128)S(1)} %collective-permute-done.34.refs_3_, f32[1024,2048]{1,0:T(8,128)S(1)} %get-tuple-element.89.refs_4_, ...), custom_call_target="tpu_custom_call" | custom-call | flops 4000000000 | tf_op jit(solution)/shard_map/pallas_call | solution.py:36
  (34 shorter events, 0.1 us)
Async XLA Ops:
  0.6 36.1 %copy-start.1 = (bf16[1024,128]{1,0:T(8,128)(2,1)S(1)}, bf16[1024,128]{1,0:T(8,128)(2,1)}, u32[]{:S(2)}) copy-start(bf16[1024,128]{1,0:T(8,128)(2,1)} %refs_0_.2) | copy-start | bytes 786436
  0.6 33.1 %copy-start = (bf16[1024,128]{1,0:T(8,128)(2,1)S(1)}, bf16[1024,128]{1,0:T(8,128)(2,1)}, u32[]{:S(2)}) copy-start(bf16[1024,128]{1,0:T(8,128)(2,1)} %refs_0_.3) | copy-start | bytes 786436
  0.6 16.0 %collective-permute-start.7 = (bf16[1024,128]{1,0:T(8,128)(2,1)}, bf16[1024,128]{1,0:T(8,128)(2,1)S(1)}, u32[]{:S(2)}, u32[]{:S(2)}) collective-permute-start(bf16[1024,128]{1,0:T(8,128)(2,1)} %refs_0_.2), channel_id=1, source_target_pairs={{0,2},{1,3},{2,0},{3,1},{4,6},{5,7},{6,4},{7,5},{8,10},{9,11},{10,... | collective-permute-start | bytes 786440 | tf_op jit(solution)/shard_map/ppermute | solution.py:473
  3.8 16.0 %collective-permute-start.3 = (bf16[1024,128]{1,0:T(8,128)(2,1)}, bf16[1024,128]{1,0:T(8,128)(2,1)S(1)}, u32[]{:S(2)}, u32[]{:S(2)}) collective-permute-start(bf16[1024,128]{1,0:T(8,128)(2,1)} %refs_0_.2), channel_id=1, source_target_pairs={{0,4},{1,5},{2,6},{3,7},{4,0},{5,1},{6,2},{7,3},{8,12},{9,13},{10,... | collective-permute-start | bytes 786440 | tf_op jit(solution)/shard_map/ppermute | solution.py:473
  6.4 27.4 %collective-permute-start.8 = (bf16[1024,128]{1,0:T(8,128)(2,1)}, bf16[1024,128]{1,0:T(8,128)(2,1)S(1)}, u32[]{:S(2)}, u32[]{:S(2)}) collective-permute-start(bf16[1024,128]{1,0:T(8,128)(2,1)} %refs_0_.2), channel_id=1, source_target_pairs={{0,1},{1,0},{2,3},{3,2},{4,5},{5,4},{6,7},{7,6},{8,9},{9,8},{10,11... | collective-permute-start | bytes 786440 | tf_op jit(solution)/shard_map/ppermute | solution.py:473
  6.4 53.0 %collective-permute-start = (bf16[1024,128]{1,0:T(8,128)(2,1)}, bf16[1024,128]{1,0:T(8,128)(2,1)S(1)}, u32[]{:S(2)}, u32[]{:S(2)}) collective-permute-start(bf16[1024,128]{1,0:T(8,128)(2,1)} %refs_0_.3), channel_id=1, source_target_pairs={{0,2},{1,3},{2,0},{3,1},{4,6},{5,7},{6,4},{7,5},{8,10},{9,11},{10,... | collective-permute-start | bytes 786440 | tf_op jit(solution)/shard_map/ppermute | solution.py:473
  6.8 52.6 %collective-permute-start.1 = (bf16[1024,128]{1,0:T(8,128)(2,1)}, bf16[1024,128]{1,0:T(8,128)(2,1)S(1)}, u32[]{:S(2)}, u32[]{:S(2)}) collective-permute-start(bf16[1024,128]{1,0:T(8,128)(2,1)} %refs_0_.3), channel_id=1, source_target_pairs={{0,4},{1,5},{2,6},{3,7},{4,0},{5,1},{6,2},{7,3},{8,12},{9,13},{10,... | collective-permute-start | bytes 786440 | tf_op jit(solution)/shard_map/ppermute | solution.py:473
  16.6 19.6 %collective-permute-start.9 = (bf16[1024,128]{1,0:T(8,128)(2,1)S(1)}, bf16[1024,128]{1,0:T(8,128)(2,1)S(1)}, u32[]{:S(2)}, u32[]{:S(2)}) collective-permute-start(bf16[1024,128]{1,0:T(8,128)(2,1)S(1)} %collective-permute-done.7.refs_1_), channel_id=1, source_target_pairs={{0,1},{1,0},{2,3},{3,2},{4,5},{5,4},{6,7},{7,6},{8,9},{9,8},{10,11... | collective-permute-start | bytes 786440 | tf_op jit(solution)/shard_map/ppermute | solution.py:473
  19.8 16.5 %collective-permute-start.4 = (bf16[1024,128]{1,0:T(8,128)(2,1)S(1)}, bf16[1024,128]{1,0:T(8,128)(2,1)S(1)}, u32[]{:S(2)}, u32[]{:S(2)}) collective-permute-start(bf16[1024,128]{1,0:T(8,128)(2,1)S(1)} %collective-permute-done.3.refs_0_), channel_id=1, source_target_pairs={{0,2},{1,3},{2,0},{3,1},{4,6},{5,7},{6,4},{7,5},{8,10},{9,11},{10,... | collective-permute-start | bytes 786440 | tf_op jit(solution)/shard_map/ppermute | solution.py:473
  33.8 25.7 %collective-permute-start.2 = (bf16[1024,128]{1,0:T(8,128)(2,1)S(1)}, bf16[1024,128]{1,0:T(8,128)(2,1)S(1)}, u32[]{:S(2)}, u32[]{:S(2)}) collective-permute-start(bf16[1024,128]{1,0:T(8,128)(2,1)S(1)} %copy-done), channel_id=1, source_target_pairs={{0,6},{1,7},{2,4},{3,5},{4,2},{5,3},{6,0},{7,1},{8,14},{9,15},{10,... | collective-permute-start | bytes 786440 | tf_op jit(solution)/shard_map/ppermute | solution.py:473
  36.2 11.3 %collective-permute-start.5 = (bf16[1024,128]{1,0:T(8,128)(2,1)S(1)}, bf16[1024,128]{1,0:T(8,128)(2,1)S(1)}, u32[]{:S(2)}, u32[]{:S(2)}) collective-permute-start(bf16[1024,128]{1,0:T(8,128)(2,1)S(1)} %collective-permute-done.3.refs_0_), channel_id=1, source_target_pairs={{0,1},{1,0},{2,3},{3,2},{4,5},{5,4},{6,7},{7,6},{8,9},{9,8},{10,11... | collective-permute-start | bytes 786440 | tf_op jit(solution)/shard_map/ppermute | solution.py:473
  36.3 11.5 %collective-permute-start.6 = (bf16[1024,128]{1,0:T(8,128)(2,1)S(1)}, bf16[1024,128]{1,0:T(8,128)(2,1)S(1)}, u32[]{:S(2)}, u32[]{:S(2)}) collective-permute-start(bf16[1024,128]{1,0:T(8,128)(2,1)S(1)} %collective-permute-done.4.refs_1_), channel_id=1, source_target_pairs={{0,1},{1,0},{2,3},{3,2},{4,5},{5,4},{6,7},{7,6},{8,9},{9,8},{10,11... | collective-permute-start | bytes 786440 | tf_op jit(solution)/shard_map/ppermute | solution.py:473
  47.6 15.3 %collective-permute-start.13 = (bf16[1024,128]{1,0:T(8,128)(2,1)S(1)}, bf16[1024,128]{1,0:T(8,128)(2,1)S(1)}, u32[]{:S(2)}, u32[]{:S(2)}) collective-permute-start(bf16[1024,128]{1,0:T(8,128)(2,1)S(1)} %copy-done), channel_id=1, source_target_pairs={{0,1},{1,0},{2,3},{3,2},{4,5},{5,4},{6,7},{7,6},{8,9},{9,8},{10,11... | collective-permute-start | bytes 786440 | tf_op jit(solution)/shard_map/ppermute | solution.py:473
  59.4 4.0 %collective-permute-start.14 = (bf16[1024,128]{1,0:T(8,128)(2,1)S(1)}, bf16[1024,128]{1,0:T(8,128)(2,1)S(1)}, u32[]{:S(2)}, u32[]{:S(2)}) collective-permute-start(bf16[1024,128]{1,0:T(8,128)(2,1)S(1)} %collective-permute-done.refs_1_), channel_id=1, source_target_pairs={{0,1},{1,0},{2,3},{3,2},{4,5},{5,4},{6,7},{7,6},{8,9},{9,8},{10,11... | collective-permute-start | bytes 786440 | tf_op jit(solution)/shard_map/ppermute | solution.py:473
  59.9 4.0 %collective-permute-start.15 = (bf16[1024,128]{1,0:T(8,128)(2,1)S(1)}, bf16[1024,128]{1,0:T(8,128)(2,1)S(1)}, u32[]{:S(2)}, u32[]{:S(2)}) collective-permute-start(bf16[1024,128]{1,0:T(8,128)(2,1)S(1)} %collective-permute-done.1.refs_2_), channel_id=1, source_target_pairs={{0,1},{1,0},{2,3},{3,2},{4,5},{5,4},{6,7},{7,6},{8,9},{9,8},{10,11... | collective-permute-start | bytes 786440 | tf_op jit(solution)/shard_map/ppermute | solution.py:473
  60.0 3.9 %collective-permute-start.16 = (bf16[1024,128]{1,0:T(8,128)(2,1)S(1)}, bf16[1024,128]{1,0:T(8,128)(2,1)S(1)}, u32[]{:S(2)}, u32[]{:S(2)}) collective-permute-start(bf16[1024,128]{1,0:T(8,128)(2,1)S(1)} %collective-permute-done.2.refs_3_), channel_id=1, source_target_pairs={{0,1},{1,0},{2,3},{3,2},{4,5},{5,4},{6,7},{7,6},{8,9},{9,8},{10,11... | collective-permute-start | bytes 786440 | tf_op jit(solution)/shard_map/ppermute | solution.py:473
  60.4 12.0 %collective-permute-start.12 = (f32[1,8192]{1,0:T(1,128)S(1)}, f32[1,8192]{1,0:T(1,128)S(1)}, u32[]{:S(2)}, u32[]{:S(2)}) collective-permute-start(f32[1,8192]{1,0:T(1,128)S(1)} %get-tuple-element.76.refs_0_), channel_id=1, source_target_pairs={{0,24},{8,16},{16,8},{24,0},{1,25},{9,17},{17,9},{25,1},{2,26},{10... | collective-permute-start | bytes 98312 | tf_op jit(solution)/shard_map/ppermute | solution.py:473
  62.9 9.6 %collective-permute-start.10 = (f32[1,8192]{1,0:T(1,128)S(1)}, f32[1,8192]{1,0:T(1,128)S(1)}, u32[]{:S(2)}, u32[]{:S(2)}) collective-permute-start(f32[1,8192]{1,0:T(1,128)S(1)} %get-tuple-element.76.refs_0_), channel_id=1, source_target_pairs={{0,8},{8,0},{16,24},{24,16},{1,9},{9,1},{17,25},{25,17},{2,10},{10... | collective-permute-start | bytes 98312 | tf_op jit(solution)/shard_map/ppermute | solution.py:473
  63.4 9.1 %collective-permute-start.11 = (f32[1,8192]{1,0:T(1,128)S(1)}, f32[1,8192]{1,0:T(1,128)S(1)}, u32[]{:S(2)}, u32[]{:S(2)}) collective-permute-start(f32[1,8192]{1,0:T(1,128)S(1)} %get-tuple-element.76.refs_0_), channel_id=1, source_target_pairs={{0,16},{8,24},{16,0},{24,8},{1,17},{9,25},{17,1},{25,9},{2,18},{10... | collective-permute-start | bytes 98312 | tf_op jit(solution)/shard_map/ppermute | solution.py:473
  75.5 1.2 collective-permute-start.17
  76.6 12.1 %collective-permute-start.20 = (f32[8,128]{1,0:T(8,128)S(1)}, f32[8,128]{1,0:T(8,128)S(1)}, u32[]{:S(2)}, u32[]{:S(2)}) collective-permute-start(f32[8,128]{1,0:T(8,128)S(1)} %add.18.refs_0_), channel_id=1, source_target_pairs={{0,6},{1,7},{2,4},{3,5},{4,2},{5,3},{6,0},{7,1},{8,14},{9,15},{10,... | collective-permute-start | bytes 12296 | tf_op jit(solution)/shard_map/ppermute | solution.py:473
  78.1 10.7 %collective-permute-start.18 = (f32[8,128]{1,0:T(8,128)S(1)}, f32[8,128]{1,0:T(8,128)S(1)}, u32[]{:S(2)}, u32[]{:S(2)}) collective-permute-start(f32[8,128]{1,0:T(8,128)S(1)} %add.18.refs_0_), channel_id=1, source_target_pairs={{0,2},{1,3},{2,0},{3,1},{4,6},{5,7},{6,4},{7,5},{8,10},{9,11},{10,... | collective-permute-start | bytes 12296 | tf_op jit(solution)/shard_map/ppermute | solution.py:473
  78.2 10.5 %collective-permute-start.19 = (f32[8,128]{1,0:T(8,128)S(1)}, f32[8,128]{1,0:T(8,128)S(1)}, u32[]{:S(2)}, u32[]{:S(2)}) collective-permute-start(f32[8,128]{1,0:T(8,128)S(1)} %add.18.refs_0_), channel_id=1, source_target_pairs={{0,4},{1,5},{2,6},{3,7},{4,0},{5,1},{6,2},{7,3},{8,12},{9,13},{10,... | collective-permute-start | bytes 12296 | tf_op jit(solution)/shard_map/ppermute | solution.py:473
  91.6 11.2 %collective-permute-start.23 = (f32[1,8192]{1,0:T(1,128)S(1)}, f32[1,8192]{1,0:T(1,128)S(1)}, u32[]{:S(2)}, u32[]{:S(2)}) collective-permute-start(f32[1,8192]{1,0:T(1,128)S(1)} %shard_map.59.refs_0_), channel_id=1, source_target_pairs={{0,24},{8,16},{16,8},{24,0},{1,25},{9,17},{17,9},{25,1},{2,26},{10... | collective-permute-start | bytes 98312 | tf_op jit(solution)/shard_map/ppermute | solution.py:473
  94.1 8.8 %collective-permute-start.21 = (f32[1,8192]{1,0:T(1,128)S(1)}, f32[1,8192]{1,0:T(1,128)S(1)}, u32[]{:S(2)}, u32[]{:S(2)}) collective-permute-start(f32[1,8192]{1,0:T(1,128)S(1)} %shard_map.59.refs_0_), channel_id=1, source_target_pairs={{0,8},{8,0},{16,24},{24,16},{1,9},{9,1},{17,25},{25,17},{2,10},{10... | collective-permute-start | bytes 98312 | tf_op jit(solution)/shard_map/ppermute | solution.py:473
  94.7 8.2 %collective-permute-start.22 = (f32[1,8192]{1,0:T(1,128)S(1)}, f32[1,8192]{1,0:T(1,128)S(1)}, u32[]{:S(2)}, u32[]{:S(2)}) collective-permute-start(f32[1,8192]{1,0:T(1,128)S(1)} %shard_map.59.refs_0_), channel_id=1, source_target_pairs={{0,16},{8,24},{16,0},{24,8},{1,17},{9,25},{17,1},{25,9},{2,18},{10... | collective-permute-start | bytes 98312 | tf_op jit(solution)/shard_map/ppermute | solution.py:473
  105.9 1.2 collective-permute-start.24
  107.0 8.2 %collective-permute-start.27 = (f32[8,128]{1,0:T(8,128)S(1)}, f32[8,128]{1,0:T(8,128)S(1)}, u32[]{:S(2)}, u32[]{:S(2)}) collective-permute-start(f32[8,128]{1,0:T(8,128)S(1)} %add.19.refs_0_), channel_id=1, source_target_pairs={{0,6},{1,7},{2,4},{3,5},{4,2},{5,3},{6,0},{7,1},{8,14},{9,15},{10,... | collective-permute-start | bytes 12296 | tf_op jit(solution)/shard_map/ppermute | solution.py:473
  108.4 6.8 %collective-permute-start.25 = (f32[8,128]{1,0:T(8,128)S(1)}, f32[8,128]{1,0:T(8,128)S(1)}, u32[]{:S(2)}, u32[]{:S(2)}) collective-permute-start(f32[8,128]{1,0:T(8,128)S(1)} %add.19.refs_0_), channel_id=1, source_target_pairs={{0,2},{1,3},{2,0},{3,1},{4,6},{5,7},{6,4},{7,5},{8,10},{9,11},{10,... | collective-permute-start | bytes 12296 | tf_op jit(solution)/shard_map/ppermute | solution.py:473
  108.4 6.8 %collective-permute-start.26 = (f32[8,128]{1,0:T(8,128)S(1)}, f32[8,128]{1,0:T(8,128)S(1)}, u32[]{:S(2)}, u32[]{:S(2)}) collective-permute-start(f32[8,128]{1,0:T(8,128)S(1)} %add.19.refs_0_), channel_id=1, source_target_pairs={{0,4},{1,5},{2,6},{3,7},{4,0},{5,1},{6,2},{7,3},{8,12},{9,13},{10,... | collective-permute-start | bytes 12296 | tf_op jit(solution)/shard_map/ppermute | solution.py:473
  118.1 7.3 %collective-permute-start.30 = (f32[1,8192]{1,0:T(1,128)S(1)}, f32[1,8192]{1,0:T(1,128)S(1)}, u32[]{:S(2)}, u32[]{:S(2)}) collective-permute-start(f32[1,8192]{1,0:T(1,128)S(1)} %shard_map.64.refs_0_), channel_id=1, source_target_pairs={{0,24},{8,16},{16,8},{24,0},{1,25},{9,17},{17,9},{25,1},{2,26},{10... | collective-permute-start | bytes 98312 | tf_op jit(solution)/shard_map/ppermute | solution.py:473
  120.6 4.8 %collective-permute-start.28 = (f32[1,8192]{1,0:T(1,128)S(1)}, f32[1,8192]{1,0:T(1,128)S(1)}, u32[]{:S(2)}, u32[]{:S(2)}) collective-permute-start(f32[1,8192]{1,0:T(1,128)S(1)} %shard_map.64.refs_0_), channel_id=1, source_target_pairs={{0,8},{8,0},{16,24},{24,16},{1,9},{9,1},{17,25},{25,17},{2,10},{10... | collective-permute-start | bytes 98312 | tf_op jit(solution)/shard_map/ppermute | solution.py:473
  121.1 4.3 %collective-permute-start.29 = (f32[1,8192]{1,0:T(1,128)S(1)}, f32[1,8192]{1,0:T(1,128)S(1)}, u32[]{:S(2)}, u32[]{:S(2)}) collective-permute-start(f32[1,8192]{1,0:T(1,128)S(1)} %shard_map.64.refs_0_), channel_id=1, source_target_pairs={{0,16},{8,24},{16,0},{24,8},{1,17},{9,25},{17,1},{25,9},{2,18},{10... | collective-permute-start | bytes 98312 | tf_op jit(solution)/shard_map/ppermute | solution.py:473
  134.9 1.2 collective-permute-start.31
  136.1 4.4 %collective-permute-start.32 = (f32[24,128]{1,0:T(8,128)S(1)}, f32[24,128]{1,0:T(8,128)S(1)}, u32[]{:S(2)}, u32[]{:S(2)}) collective-permute-start(f32[24,128]{1,0:T(8,128)S(1)} %add.20.refs_0_), channel_id=1, source_target_pairs={{0,2},{1,3},{2,0},{3,1},{4,6},{5,7},{6,4},{7,5},{8,10},{9,11},{10,... | collective-permute-start | bytes 36872 | tf_op jit(solution)/shard_map/ppermute | solution.py:473
  136.1 4.6 %collective-permute-start.33 = (f32[24,128]{1,0:T(8,128)S(1)}, f32[24,128]{1,0:T(8,128)S(1)}, u32[]{:S(2)}, u32[]{:S(2)}) collective-permute-start(f32[24,128]{1,0:T(8,128)S(1)} %add.20.refs_0_), channel_id=1, source_target_pairs={{0,4},{1,5},{2,6},{3,7},{4,0},{5,1},{6,2},{7,3},{8,12},{9,13},{10,... | collective-permute-start | bytes 36872 | tf_op jit(solution)/shard_map/ppermute | solution.py:473
  138.1 5.5 %collective-permute-start.34 = (f32[24,128]{1,0:T(8,128)S(1)}, f32[24,128]{1,0:T(8,128)S(1)}, u32[]{:S(2)}, u32[]{:S(2)}) collective-permute-start(f32[24,128]{1,0:T(8,128)S(1)} %add.20.refs_0_), channel_id=1, source_target_pairs={{0,6},{1,7},{2,4},{3,5},{4,2},{5,3},{6,0},{7,1},{8,14},{9,15},{10,... | collective-permute-start | bytes 36872 | tf_op jit(solution)/shard_map/ppermute | solution.py:473
